TPU v7x, 128 devices: a whole 4x4x4 slice. The times are simulated.
128 devices in a mesh: gx: 16 (over z, x), gy: 4 (over y_hi, core), gz: 2 (over y_lo).
Axes of the slice: x: 4, y: 4 (y_hi: 2, y_lo: 2; y = y_hi * 2 + y_lo), z: 4, core: 2. Of those that a mesh axis runs over, the one named last changes fastest.
Arguments:
- hidden: bfloat16 [49152, 4608], P(('gx', 'gy', 'gz')), may hold values from -24 to 24
- out_grad: bfloat16 [49152, 1152], P(('gx', 'gy', 'gz')), may hold values from -6 to 6
- down_weight: bfloat16 [4608, 1152], replicated, may hold values from -0.1875 to 0.1875
Outputs:
- weight_grad: float32 [4608, 1152], P(('gx', 'gy', 'gz'))
- hidden_grad: bfloat16 [49152, 4608], P(('gx', 'gy', 'gz'))
All inputs are finite; a program needn't handle non-finite values.
Results may differ from a plain program's by a relative error of at most 0.001.
Values may be sent and summed in bfloat16 or wider, within the bound.
No kernel may reach another device: no remote copies, remote signals or barrier semaphores. Data moves between devices by JAX's collectives and lax.ppermute only.
A program may use at most 128 MiB of HBM per device.

v0:
```python
import functools

import jax
import jax.numpy as jnp
from jax import lax
from jax.experimental import pallas as pl
from jax.experimental.pallas import tpu as pltpu
from jax.sharding import PartitionSpec as P


AXES = ("gx", "gy", "gz")
SIDE = 4
BLOCK = 36
PADDED = 40
TAIL = 8
WIDE = 768
NARROW = 384


def near(array):
    return pltpu.with_memory_space_constraint(array, pltpu.VMEM)


def position(index):
    return index >> 5, index >> 3 & 3, index >> 1 & 2 | index & 1, index >> 1 & 1


def device(z, x, y, core):
    return ((z * 4 + x) * 4 + y // 2 * 2 + core) * 2 + y % 2


def routes(dims, step):
    pairs = []
    for source in range(128):
        at = dict(zip("zxyc", position(source)))
        along = dims[at["c"]]
        at[along] = (at[along] + step) % SIDE
        pairs.append((source, device(at["z"], at["x"], at["y"], at["c"])))
    return pairs


def across_cores(array):
    pairs = []
    for source in range(128):
        z, x, y, core = position(source)
        pairs.append((source, device(z, x, y, 1 - core)))
    return lax.ppermute(array, AXES, pairs)


def turn_body(where, hidden, send, keep):
    core = position(where[0])[3]
    turned = hidden[...].T
    for x in range(SIDE):
        rows = 288 * x
        piece = jnp.concatenate([turned[rows : rows + 72], turned[rows + 144 : rows + 216]], 0)

        @pl.when(core == 0)
        def _():
            keep[x] = piece

        @pl.when(core == 1)
        def _():
            send[x] = piece

    for y in range(SIDE):
        rows = 144 * (y // 2) + 72 + BLOCK * (y % 2)
        piece = jnp.concatenate(
            [turned[288 * x + rows : 288 * x + rows + BLOCK] for x in range(SIDE)], 0
        )

        @pl.when(core == 1)
        def _():
            keep[y] = piece

        @pl.when(core == 0)
        def _():
            send[y] = piece


def turn(where, hidden):
    tokens, width = hidden.shape
    out = pltpu.VMEM((SIDE, width // 8, tokens), hidden.dtype)
    return pl.pallas_call(
        turn_body,
        grid=(SIDE,),
        in_specs=[
            pl.BlockSpec(memory_space=pltpu.SMEM),
            pl.BlockSpec((tokens, width // SIDE), lambda b: (0, b)),
        ],
        out_specs=[pl.BlockSpec((SIDE, width // 32, tokens), lambda b: (0, b, 0))] * 2,
        out_shape=[out, out],
        compiler_params=pltpu.CompilerParams(vmem_limit_bytes=16 * 2**20),
        cost_estimate=pl.CostEstimate(flops=2 * 10**9, bytes_accessed=7 * 10**6, transcendentals=0),
    )(where, pltpu.with_memory_space_constraint(hidden, pltpu.HBM))


def largest(values):
    return jnp.max(jnp.max(values, axis=0, keepdims=True).astype(jnp.float32))


def product_body(step, where, mine, other, grad, other_grad, *refs):
    if step == 1:
        wide, narrow, level = refs
        top = largest(jnp.maximum(jnp.abs(mine[...]), jnp.abs(other[...])).reshape(-1, mine.shape[2]))
        grad_top = largest(jnp.maximum(jnp.abs(grad[...]), jnp.abs(other_grad[...])))
        tokens = grad.shape[0] * 2
        bound = jnp.full((TAIL, 128), 1.0, jnp.float32)
        bound = bound * (top * grad_top * tokens)
        bits = 15.0 - jnp.ceil(jnp.log2(jnp.maximum(bound, 2.0**-60)))
        level[...] = bits
    else:
        given, wide, narrow = refs
        bits = given[...]
    scale = jnp.exp2(bits)[0:1, 0:1]
    z, x, y, core = position(where[0])
    at = jnp.where(core == 0, x, y) + step & 3
    left = jnp.concatenate([mine[at], other[at]], 1)
    both = jnp.concatenate([grad[...], other_grad[...]], 0)
    row = pl.multiple_of((z + step & 3) * 144, 16)
    cut = jnp.concatenate(
        [
            jnp.concatenate([source[t, pl.ds(row, 144)] for t in range(SIDE)], 0)
            for source in (mine, other)
        ],
        1,
    )
    one = jnp.dot(left, both[:, :WIDE], preferred_element_type=jnp.float32)
    two = jnp.dot(cut, both[:, WIDE:], preferred_element_type=jnp.float32)
    wide[0:576] = one * scale if step else one
    narrow[0:576] = two * scale if step else two
    wide[576:] = jnp.broadcast_to(bits[:, 0:1], (TAIL, WIDE))
    narrow[576:] = jnp.broadcast_to(bits[:, 0:1], (TAIL, NARROW))


def product(step, where, mine, other, grad, other_grad, level=None):
    first = step == 1
    outs = [
        pltpu.VMEM((576 + TAIL, WIDE), jnp.float32),
        pltpu.VMEM((576 + TAIL, NARROW), jnp.float32),
    ]
    if first:
        outs.append(pltpu.VMEM((TAIL, 128), jnp.float32))
    n = 4 if first else 5
    return pl.pallas_call(
        functools.partial(product_body, step),
        in_specs=[pl.BlockSpec(memory_space=pltpu.SMEM)] + [pl.BlockSpec(memory_space=pltpu.VMEM)] * n,
        out_specs=[pl.BlockSpec(memory_space=pltpu.VMEM)] * len(outs),
        out_shape=outs,
        compiler_params=pltpu.CompilerParams(vmem_limit_bytes=16 * 2**20),
        cost_estimate=pl.CostEstimate(flops=10**9, bytes_accessed=5 * 10**6, transcendentals=0),
    )(where, *map(near, [mine, other, grad, other_grad] + ([] if first else [level])))


def power(part, rows):
    return jnp.exp2(-part[rows : rows + 1].astype(jnp.float32))


def total(own, parts, rows):
    value = own[0:rows]
    for part in parts:
        value = value + part[0:rows].astype(jnp.float32) * power(part, rows)
    return value


def spread_body(blocks, stride, where, *refs):
    z, x, y, core = position(where[0])
    if blocks == 16:
        ways = (
            (jnp.where(core == 0, z, x), jnp.where(core == 0, 4, 1), jnp.where(core == 0, 1, 4)),
            (y, jnp.where(core == 0, 1, 4), jnp.where(core == 0, 4, 1)),
        )
    else:
        ways = ((jnp.where(core == 0, y, z), 1, 0), (x, 1, 0))
    for p, width in enumerate((WIDE, NARROW)):
        value, tails, out, scratch = refs[p], refs[2 + p], refs[4 + p], refs[6 + p]
        bits = jnp.min(tails[...], axis=0, keepdims=True) - 2.0
        scale = jnp.exp2(bits)[0:1, 0:1]
        for i in range(blocks):
            scratch[i, 0:BLOCK] = value[stride * i : stride * i + BLOCK]
            scratch[i, BLOCK:] = jnp.zeros((PADDED - BLOCK, width), jnp.float32)
        at, major, minor = ways[p]
        for k in range(SIDE):
            chunk = at + k & 3
            for t in range(blocks // SIDE):
                piece = scratch[chunk * major + t * minor]
                out[k, PADDED * t : PADDED * (t + 1)] = piece * scale if k else piece
            out[k, PADDED * blocks // SIDE :] = jnp.broadcast_to(bits[:, 0:1], (TAIL, width))


def spread(where, blocks, stride, wide, narrow, own_bits):
    high = PADDED * blocks // SIDE + TAIL
    rows = stride * blocks
    inputs = [total(*pair, rows) for pair in (wide, narrow)]
    for p, (_, parts) in enumerate((wide, narrow)):
        tails = [part[rows:, 0:128].astype(jnp.float32) for part in parts]
        inputs.append(jnp.concatenate([own_bits[p], *tails], 0))
    return pl.pallas_call(
        functools.partial(spread_body, blocks, stride),
        in_specs=[pl.BlockSpec(memory_space=pltpu.SMEM)] + [pl.BlockSpec(memory_space=pltpu.VMEM)] * 4,
        out_specs=[pl.BlockSpec(memory_space=pltpu.VMEM)] * 2,
        out_shape=[
            pltpu.VMEM((SIDE, high, WIDE), jnp.float32),
            pltpu.VMEM((SIDE, high, NARROW), jnp.float32),
        ],
        scratch_shapes=[
            pltpu.VMEM((blocks, PADDED, WIDE), jnp.float32),
            pltpu.VMEM((blocks, PADDED, NARROW), jnp.float32),
        ],
        compiler_params=pltpu.CompilerParams(vmem_limit_bytes=12 * 2**20),
        cost_estimate=pl.CostEstimate(flops=10**8, bytes_accessed=10**7, transcendentals=0),
    )(where, *map(near, inputs))


def exchange(chunks, dims):
    arrived = {}
    for k in chunks:
        arrived[k] = lax.ppermute(chunks[k].astype(jnp.float16), AXES, routes(dims, k))
    return arrived


def input_gradient_body(grad, weight, out):
    out[...] = lax.dot_general(
        grad[...], weight[...], (((1,), (1,)), ((), ())), preferred_element_type=jnp.float32
    ).astype(out.dtype)


def input_gradient(grad, weight):
    tokens, width = grad.shape
    features = weight.shape[0]
    step = 512
    return pl.pallas_call(
        input_gradient_body,
        grid=(features // step,),
        in_specs=[
            pl.BlockSpec((tokens, width), lambda i: (0, 0)),
            pl.BlockSpec((step, width), lambda i: (i, 0)),
        ],
        out_specs=pl.BlockSpec((tokens, step), lambda i: (0, i)),
        out_shape=pltpu.HBM((tokens, features), grad.dtype),
        compiler_params=pltpu.CompilerParams(vmem_limit_bytes=16 * 2**20),
        cost_estimate=pl.CostEstimate(
            flops=2 * tokens * width * features, bytes_accessed=15 * 10**6, transcendentals=0
        ),
    )(grad, pltpu.with_memory_space_constraint(weight, pltpu.HBM))


def listed(parts):
    return [parts[k] for k in (1, 2, 3)]


def body(hidden, out_grad, down_weight):
    where = lax.axis_index(AXES).reshape(1)
    tokens = hidden.shape[0] * 128
    factor = 1.0 / float(tokens) ** 0.5

    other_grad = across_cores(out_grad)
    send, keep = turn(where, hidden)
    got = across_cores(send)

    level = None
    wide, narrow = {}, {}
    from_wide, from_narrow = {}, {}
    for k in (1, 3, 2, 0):
        outs = product(k, where, keep, got, out_grad, other_grad, level)
        if level is None:
            level = outs[2]
        wide[k], narrow[k] = outs[0], outs[1]
        if k:
            from_wide |= exchange({k: wide[k]}, "xy")
            from_narrow |= exchange({k: narrow[k]}, "zz")

    hidden_grad = input_gradient(out_grad, down_weight)

    wide, narrow = spread(
        where, 16, BLOCK, (wide[0], listed(from_wide)), (narrow[0], listed(from_narrow)), (level, level)
    )
    from_wide = exchange({k: wide[k] for k in (1, 3, 2)}, "zx")
    from_narrow = exchange({k: narrow[k] for k in (1, 3, 2)}, "yy")

    own_bits = (wide[0, 160:, 0:128], narrow[0, 160:, 0:128])
    wide, narrow = spread(
        where, 4, PADDED, (wide[0], listed(from_wide)), (narrow[0], listed(from_narrow)), own_bits
    )
    from_wide = exchange({k: wide[k] for k in (1, 3, 2)}, "yz")
    from_narrow = exchange({k: narrow[k] for k in (1, 3, 2)}, "xx")

    sums = [
        total(own[0], listed(parts), PADDED)[0:BLOCK]
        for own, parts in ((wide, from_wide), (narrow, from_narrow))
    ]
    weight_grad = jnp.concatenate(sums, 1) * factor
    return (weight_grad, hidden_grad)


def solution(mesh):
    in_specs = (P(AXES, None), P(AXES, None), P())
    out_specs = (P(AXES, None), P(AXES, None))
    return jax.shard_map(body, mesh=mesh, in_specs=in_specs, out_specs=out_specs, check_vma=False)
```

profile of v0, /device:TPU:6, one launch (start us, length us, event | category | flops | bytes accessed | tf_op | source)
XLA Modules:
  0.0 87.6 jit_solution(3497462987273055061)
XLA Ops:
  0.6 4.1 %shard_map.50 = (bf16[4,576,384]{2,1,0:T(8,128)(2,1)S(1)}, bf16[4,576,384]{2,1,0:T(8,128)(2,1)S(1)}) custom-call(s32[1]{0:T(128)} %bitcast.where, bf16[384,4608]{1,0:T(8,128)(2,1)} %hidden.1), custom_call_target="tpu_custom_call" | custom-call | flops 2000000000 | bytes 7000000 | tf_op jit(solution)/shard_map/pallas_call | solution.py:83
  4.8 0.5 collective-permute-start.1
  5.3 4.4 %collective-permute-done.1.other_grad = bf16[384,1152]{1,0:T(8,128)(2,1)S(1)} collective-permute-done((bf16[384,1152]{1,0:T(8,128)(2,1)S(1)}, bf16[384,1152]{1,0:T(8,128)(2,1)S(1)}, u32[]{:S(2)}, u32[]{:S(2)}) %collective-permute-start.1) | collective-permute-done | bytes 884768 | tf_op jit(solution)/shard_map/ppermute | solution.py:47
  9.8 1.6 %shard_map.51 = (f32[584,768]{1,0:T(8,128)S(1)}, f32[584,384]{1,0:T(8,128)S(1)}, f32[8,128]{1,0:T(8,128)S(1)}) custom-call(s32[1]{0:T(128)} %bitcast.where, bf16[4,576,384]{2,1,0:T(8,128)(2,1)S(1)} %get-tuple-element.17.mine, bf16[4,576,384]{2,1,0:T(8,128)(2,1)S(1)} %collective-permute-done.other, bf16[384,1152]{1,0:T(8,128)(2,1)S(1)} %copy-done, ...), custom_call_target="tpu_custom_call" | custom-call | flops 1000000000 | bytes 5000000 | tf_op jit(solution)/shard_map/pallas_call | solution.py:144
  11.4 1.3 %shard_map.53 = (f32[584,768]{1,0:T(8,128)S(1)}, f32[584,384]{1,0:T(8,128)S(1)}) custom-call(s32[1]{0:T(128)} %bitcast.where, bf16[4,576,384]{2,1,0:T(8,128)(2,1)S(1)} %get-tuple-element.17.mine, bf16[4,576,384]{2,1,0:T(8,128)(2,1)S(1)} %collective-permute-done.other, bf16[384,1152]{1,0:T(8,128)(2,1)S(1)} %copy-done, ...), custom_call_target="tpu_custom_call" | custom-call | flops 1000000000 | bytes 5000000 | tf_op jit(solution)/shard_map/pallas_call | solution.py:144
  12.8 4.0 %collective-permute-start.6 = (f16[584,384]{1,0:T(8,128)(2,1)S(1)}, f16[584,384]{1,0:T(8,128)(2,1)S(1)}, u32[]{:S(2)}, u32[]{:S(2)}) collective-permute-start(f16[584,384]{1,0:T(8,128)(2,1)S(1)} %convert_element_type.222), channel_id=1, source_target_pairs={{0,64},{1,65},{2,66},{3,67},{4,68},{5,69},{6,70},{7,71},{8,72},{9,... | collective-permute-start | bytes 1345544 | tf_op jit(solution)/shard_map/ppermute | solution.py:217
  16.7 1.3 %shard_map.54 = (f32[584,768]{1,0:T(8,128)S(1)}, f32[584,384]{1,0:T(8,128)S(1)}) custom-call(s32[1]{0:T(128)} %bitcast.where, bf16[4,576,384]{2,1,0:T(8,128)(2,1)S(1)} %get-tuple-element.17.mine, bf16[4,576,384]{2,1,0:T(8,128)(2,1)S(1)} %collective-permute-done.other, bf16[384,1152]{1,0:T(8,128)(2,1)S(1)} %copy-done, ...), custom_call_target="tpu_custom_call" | custom-call | flops 1000000000 | bytes 5000000 | tf_op jit(solution)/shard_map/pallas_call | solution.py:144
  18.1 0.8 collective-permute-start.7
  18.9 11.4 %shard_map.57 = bf16[384,4608]{1,0:T(8,128)(2,1)} custom-call(bf16[384,1152]{1,0:T(8,128)(2,1)S(1)} %copy-done, bf16[4608,1152]{1,0:T(8,128)(2,1)} %weight.1), custom_call_target="tpu_custom_call" | custom-call | flops 4076863488 | bytes 15000000 | tf_op jit(solution)/shard_map/pallas_call | solution.py:231
  30.4 1.5 %collective-permute-start.3 = (f16[584,768]{1,0:T(8,128)(2,1)S(1)}, f16[584,768]{1,0:T(8,128)(2,1)S(1)}, u32[]{:S(2)}, u32[]{:S(2)}) collective-permute-start(f16[584,768]{1,0:T(8,128)(2,1)S(1)} %convert_element_type.213), channel_id=1, source_target_pairs={{0,16},{1,17},{2,6},{3,7},{4,20},{5,21},{6,2},{7,3},{8,24},{9,25},... | collective-permute-start | bytes 2691080 | tf_op jit(solution)/shard_map/ppermute | solution.py:217
  32.2 1.4 %collective-permute-start.5 = (f16[584,384]{1,0:T(8,128)(2,1)S(1)}, f16[584,384]{1,0:T(8,128)(2,1)S(1)}, u32[]{:S(2)}, u32[]{:S(2)}) collective-permute-start(f16[584,384]{1,0:T(8,128)(2,1)S(1)} %convert_element_type.219), channel_id=1, source_target_pairs={{0,32},{1,33},{2,34},{3,35},{4,36},{5,37},{6,38},{7,39},{8,40},{9,... | collective-permute-start | bytes 1345544 | tf_op jit(solution)/shard_map/ppermute | solution.py:217
  33.6 1.3 %shard_map.52 = (f32[584,768]{1,0:T(8,128)S(1)}, f32[584,384]{1,0:T(8,128)S(1)}) custom-call(s32[1]{0:T(128)} %bitcast.where, bf16[4,576,384]{2,1,0:T(8,128)(2,1)S(1)} %get-tuple-element.17.mine, bf16[4,576,384]{2,1,0:T(8,128)(2,1)S(1)} %collective-permute-done.other, bf16[384,1152]{1,0:T(8,128)(2,1)S(1)} %copy-done, ...), custom_call_target="tpu_custom_call" | custom-call | flops 1000000000 | bytes 5000000 | tf_op jit(solution)/shard_map/pallas_call | solution.py:144
  34.9 3.3 %collective-permute-start.2 = (f16[584,768]{1,0:T(8,128)(2,1)S(1)}, f16[584,768]{1,0:T(8,128)(2,1)S(1)}, u32[]{:S(2)}, u32[]{:S(2)}) collective-permute-start(f16[584,768]{1,0:T(8,128)(2,1)S(1)} %convert_element_type.210), channel_id=1, source_target_pairs={{0,8},{1,9},{2,3},{3,6},{4,12},{5,13},{6,7},{7,2},{8,16},{9,17},{1... | collective-permute-start | bytes 2691080 | tf_op jit(solution)/shard_map/ppermute | solution.py:217
  38.2 7.6 %collective-permute-done.5 = f16[584,384]{1,0:T(8,128)(2,1)S(1)} collective-permute-done((f16[584,384]{1,0:T(8,128)(2,1)S(1)}, f16[584,384]{1,0:T(8,128)(2,1)S(1)}, u32[]{:S(2)}, u32[]{:S(2)}) %collective-permute-start.5) | collective-permute-done | bytes 448544 | tf_op jit(solution)/shard_map/ppermute | solution.py:217
  45.9 0.3 multiply_add_fusion.1.refs_1_
  46.2 8.5 %collective-permute-done.4 = f16[584,768]{1,0:T(8,128)(2,1)S(1)} collective-permute-done((f16[584,768]{1,0:T(8,128)(2,1)S(1)}, f16[584,768]{1,0:T(8,128)(2,1)S(1)}, u32[]{:S(2)}, u32[]{:S(2)}) %collective-permute-start.4) | collective-permute-done | bytes 897056 | tf_op jit(solution)/shard_map/ppermute | solution.py:217
  54.9 0.7 multiply_add_fusion.refs_0_
  55.5 0.5 shard_map.55
  56.2 3.3 %collective-permute-start.12 = (f16[168,384]{1,0:T(8,128)(2,1)S(1)}, f16[168,384]{1,0:T(8,128)(2,1)S(1)}, u32[]{:S(2)}, u32[]{:S(2)}) collective-permute-start(f16[168,384]{1,0:T(8,128)(2,1)S(1)} %get-tuple-element.37), channel_id=1, source_target_pairs={{0,4},{1,5},{2,6},{3,7},{4,0},{5,1},{6,2},{7,3},{8,12},{9,13},{10,... | collective-permute-start | bytes 387080 | tf_op jit(solution)/shard_map/ppermute | solution.py:217
  59.4 0.7 collective-permute-start.11
  60.1 2.6 %collective-permute-start.13 = (f16[168,384]{1,0:T(8,128)(2,1)S(1)}, f16[168,384]{1,0:T(8,128)(2,1)S(1)}, u32[]{:S(2)}, u32[]{:S(2)}) collective-permute-start(f16[168,384]{1,0:T(8,128)(2,1)S(1)} %get-tuple-element.36), channel_id=1, source_target_pairs={{0,5},{1,0},{2,7},{3,2},{4,1},{5,4},{6,3},{7,6},{8,13},{9,8},{10,1... | collective-permute-start | bytes 387080 | tf_op jit(solution)/shard_map/ppermute | solution.py:217
  63.0 3.4 %collective-permute-start.9 = (f16[168,768]{1,0:T(8,128)(2,1)S(1)}, f16[168,768]{1,0:T(8,128)(2,1)S(1)}, u32[]{:S(2)}, u32[]{:S(2)}) collective-permute-start(f16[168,768]{1,0:T(8,128)(2,1)S(1)} %get-tuple-element.34), channel_id=1, source_target_pairs={{0,64},{1,65},{2,18},{3,19},{4,68},{5,69},{6,22},{7,23},{8,72},{9,... | collective-permute-start | bytes 774152 | tf_op jit(solution)/shard_map/ppermute | solution.py:217
  66.4 0.4 collective-permute-start.8
  67.0 2.3 %collective-permute-done.10 = f16[168,768]{1,0:T(8,128)(2,1)S(1)} collective-permute-done((f16[168,768]{1,0:T(8,128)(2,1)S(1)}, f16[168,768]{1,0:T(8,128)(2,1)S(1)}, u32[]{:S(2)}, u32[]{:S(2)}) %collective-permute-start.10) | collective-permute-done | bytes 258080 | tf_op jit(solution)/shard_map/ppermute | solution.py:217
  69.3 1.8 %collective-permute-done.9 = f16[168,768]{1,0:T(8,128)(2,1)S(1)} collective-permute-done((f16[168,768]{1,0:T(8,128)(2,1)S(1)}, f16[168,768]{1,0:T(8,128)(2,1)S(1)}, u32[]{:S(2)}, u32[]{:S(2)}) %collective-permute-start.9) | collective-permute-done | bytes 258080 | tf_op jit(solution)/shard_map/ppermute | solution.py:217
  71.1 2.8 %collective-permute-done.8 = f16[168,768]{1,0:T(8,128)(2,1)S(1)} collective-permute-done((f16[168,768]{1,0:T(8,128)(2,1)S(1)}, f16[168,768]{1,0:T(8,128)(2,1)S(1)}, u32[]{:S(2)}, u32[]{:S(2)}) %collective-permute-start.8) | collective-permute-done | bytes 258080 | tf_op jit(solution)/shard_map/ppermute | solution.py:217
  74.5 0.9 %collective-permute-start.19 = (f16[48,384]{1,0:T(8,128)(2,1)S(1)}, f16[48,384]{1,0:T(8,128)(2,1)S(1)}, u32[]{:S(2)}, u32[]{:S(2)}) collective-permute-start(f16[48,384]{1,0:T(8,128)(2,1)S(1)} %get-tuple-element.42), channel_id=1, source_target_pairs={{0,24},{1,25},{2,26},{3,27},{4,28},{5,29},{6,30},{7,31},{8,0},{9,1... | collective-permute-start | bytes 110600 | tf_op jit(solution)/shard_map/ppermute | solution.py:217
  75.4 1.5 %collective-permute-start.15 = (f16[48,768]{1,0:T(8,128)(2,1)S(1)}, f16[48,768]{1,0:T(8,128)(2,1)S(1)}, u32[]{:S(2)}, u32[]{:S(2)}) collective-permute-start(f16[48,768]{1,0:T(8,128)(2,1)S(1)} %get-tuple-element.40), channel_id=1, source_target_pairs={{0,4},{1,5},{2,66},{3,67},{4,0},{5,1},{6,70},{7,71},{8,12},{9,13},... | collective-permute-start | bytes 221192 | tf_op jit(solution)/shard_map/ppermute | solution.py:217
  76.9 1.8 %collective-permute-start.16 = (f16[48,768]{1,0:T(8,128)(2,1)S(1)}, f16[48,768]{1,0:T(8,128)(2,1)S(1)}, u32[]{:S(2)}, u32[]{:S(2)}) collective-permute-start(f16[48,768]{1,0:T(8,128)(2,1)S(1)} %get-tuple-element.39), channel_id=1, source_target_pairs={{0,5},{1,0},{2,98},{3,99},{4,1},{5,4},{6,102},{7,103},{8,13},{9,8}... | collective-permute-start | bytes 221192 | tf_op jit(solution)/shard_map/ppermute | solution.py:217
  78.6 2.4 %collective-permute-start.17 = (f16[48,384]{1,0:T(8,128)(2,1)S(1)}, f16[48,384]{1,0:T(8,128)(2,1)S(1)}, u32[]{:S(2)}, u32[]{:S(2)}) collective-permute-start(f16[48,384]{1,0:T(8,128)(2,1)S(1)} %get-tuple-element.41), channel_id=1, source_target_pairs={{0,8},{1,9},{2,10},{3,11},{4,12},{5,13},{6,14},{7,15},{8,16},{9,17... | collective-permute-start | bytes 110600 | tf_op jit(solution)/shard_map/ppermute | solution.py:217
  81.3 5.2 %collective-permute-done.18 = f16[48,384]{1,0:T(8,128)(2,1)S(1)} collective-permute-done((f16[48,384]{1,0:T(8,128)(2,1)S(1)}, f16[48,384]{1,0:T(8,128)(2,1)S(1)}, u32[]{:S(2)}, u32[]{:S(2)}) %collective-permute-start.18) | collective-permute-done | bytes 36896 | tf_op jit(solution)/shard_map/ppermute | solution.py:217
  86.9 0.7 maximum_multiply_fusion
  (81 shorter events, 2.6 us)
Async XLA Ops:
  0.6 4.2 %copy-start = (bf16[384,1152]{1,0:T(8,128)(2,1)S(1)}, bf16[384,1152]{1,0:T(8,128)(2,1)}, u32[]{:S(2)}) copy-start(bf16[384,1152]{1,0:T(8,128)(2,1)} %grad.9) | copy-start | bytes 2654212
  4.7 5.0 %collective-permute-start = (bf16[4,576,384]{2,1,0:T(8,128)(2,1)S(1)}, bf16[4,576,384]{2,1,0:T(8,128)(2,1)S(1)}, u32[]{:S(2)}, u32[]{:S(2)}) collective-permute-start(bf16[4,576,384]{2,1,0:T(8,128)(2,1)S(1)} %get-tuple-element.18), channel_id=1, source_target_pairs={{0,2},{1,3},{2,0},{3,1},{4,6},{5,7},{6,4},{7,5},{8,10},{9,11},{10,... | collective-permute-start | bytes 5308424 | tf_op jit(solution)/shard_map/ppermute | solution.py:47
  4.8 4.9 %collective-permute-start.1 = (bf16[384,1152]{1,0:T(8,128)(2,1)S(1)}, bf16[384,1152]{1,0:T(8,128)(2,1)S(1)}, u32[]{:S(2)}, u32[]{:S(2)}) collective-permute-start(bf16[384,1152]{1,0:T(8,128)(2,1)S(1)} %copy-done), channel_id=1, source_target_pairs={{0,2},{1,3},{2,0},{3,1},{4,6},{5,7},{6,4},{7,5},{8,10},{9,11},{10,... | collective-permute-start | bytes 2654216 | tf_op jit(solution)/shard_map/ppermute | solution.py:47
  12.8 22.2 %collective-permute-start.6 = (f16[584,384]{1,0:T(8,128)(2,1)S(1)}, f16[584,384]{1,0:T(8,128)(2,1)S(1)}, u32[]{:S(2)}, u32[]{:S(2)}) collective-permute-start(f16[584,384]{1,0:T(8,128)(2,1)S(1)} %convert_element_type.222), channel_id=1, source_target_pairs={{0,64},{1,65},{2,66},{3,67},{4,68},{5,69},{6,70},{7,71},{8,72},{9,... | collective-permute-start | bytes 1345544 | tf_op jit(solution)/shard_map/ppermute | solution.py:217
  18.1 20.1 %collective-permute-start.7 = (f16[584,384]{1,0:T(8,128)(2,1)S(1)}, f16[584,384]{1,0:T(8,128)(2,1)S(1)}, u32[]{:S(2)}, u32[]{:S(2)}) collective-permute-start(f16[584,384]{1,0:T(8,128)(2,1)S(1)} %convert_element_type.225), channel_id=1, source_target_pairs={{0,96},{1,97},{2,98},{3,99},{4,100},{5,101},{6,102},{7,103},{8,104... | collective-permute-start | bytes 1345544 | tf_op jit(solution)/shard_map/ppermute | solution.py:217
  30.4 15.8 %collective-permute-start.3 = (f16[584,768]{1,0:T(8,128)(2,1)S(1)}, f16[584,768]{1,0:T(8,128)(2,1)S(1)}, u32[]{:S(2)}, u32[]{:S(2)}) collective-permute-start(f16[584,768]{1,0:T(8,128)(2,1)S(1)} %convert_element_type.213), channel_id=1, source_target_pairs={{0,16},{1,17},{2,6},{3,7},{4,20},{5,21},{6,2},{7,3},{8,24},{9,25},... | collective-permute-start | bytes 2691080 | tf_op jit(solution)/shard_map/ppermute | solution.py:217
  32.0 22.8 %collective-permute-start.4 = (f16[584,768]{1,0:T(8,128)(2,1)S(1)}, f16[584,768]{1,0:T(8,128)(2,1)S(1)}, u32[]{:S(2)}, u32[]{:S(2)}) collective-permute-start(f16[584,768]{1,0:T(8,128)(2,1)S(1)} %convert_element_type.216), channel_id=1, source_target_pairs={{0,24},{1,25},{2,7},{3,2},{4,28},{5,29},{6,3},{7,6},{8,0},{9,1},{1... | collective-permute-start | bytes 2691080 | tf_op jit(solution)/shard_map/ppermute | solution.py:217
  32.2 13.6 %collective-permute-start.5 = (f16[584,384]{1,0:T(8,128)(2,1)S(1)}, f16[584,384]{1,0:T(8,128)(2,1)S(1)}, u32[]{:S(2)}, u32[]{:S(2)}) collective-permute-start(f16[584,384]{1,0:T(8,128)(2,1)S(1)} %convert_element_type.219), channel_id=1, source_target_pairs={{0,32},{1,33},{2,34},{3,35},{4,36},{5,37},{6,38},{7,39},{8,40},{9,... | collective-permute-start | bytes 1345544 | tf_op jit(solution)/shard_map/ppermute | solution.py:217
  34.9 19.8 %collective-permute-start.2 = (f16[584,768]{1,0:T(8,128)(2,1)S(1)}, f16[584,768]{1,0:T(8,128)(2,1)S(1)}, u32[]{:S(2)}, u32[]{:S(2)}) collective-permute-start(f16[584,768]{1,0:T(8,128)(2,1)S(1)} %convert_element_type.210), channel_id=1, source_target_pairs={{0,8},{1,9},{2,3},{3,6},{4,12},{5,13},{6,7},{7,2},{8,16},{9,17},{1... | collective-permute-start | bytes 2691080 | tf_op jit(solution)/shard_map/ppermute | solution.py:217
  56.2 10.2 %collective-permute-start.12 = (f16[168,384]{1,0:T(8,128)(2,1)S(1)}, f16[168,384]{1,0:T(8,128)(2,1)S(1)}, u32[]{:S(2)}, u32[]{:S(2)}) collective-permute-start(f16[168,384]{1,0:T(8,128)(2,1)S(1)} %get-tuple-element.37), channel_id=1, source_target_pairs={{0,4},{1,5},{2,6},{3,7},{4,0},{5,1},{6,2},{7,3},{8,12},{9,13},{10,... | collective-permute-start | bytes 387080 | tf_op jit(solution)/shard_map/ppermute | solution.py:217
  59.4 7.4 %collective-permute-start.11 = (f16[168,384]{1,0:T(8,128)(2,1)S(1)}, f16[168,384]{1,0:T(8,128)(2,1)S(1)}, u32[]{:S(2)}, u32[]{:S(2)}) collective-permute-start(f16[168,384]{1,0:T(8,128)(2,1)S(1)} %get-tuple-element.35), channel_id=1, source_target_pairs={{0,1},{1,4},{2,3},{3,6},{4,5},{5,0},{6,7},{7,2},{8,9},{9,12},{10,1... | collective-permute-start | bytes 387080 | tf_op jit(solution)/shard_map/ppermute | solution.py:217
  60.1 6.8 %collective-permute-start.13 = (f16[168,384]{1,0:T(8,128)(2,1)S(1)}, f16[168,384]{1,0:T(8,128)(2,1)S(1)}, u32[]{:S(2)}, u32[]{:S(2)}) collective-permute-start(f16[168,384]{1,0:T(8,128)(2,1)S(1)} %get-tuple-element.36), channel_id=1, source_target_pairs={{0,5},{1,0},{2,7},{3,2},{4,1},{5,4},{6,3},{7,6},{8,13},{9,8},{10,1... | collective-permute-start | bytes 387080 | tf_op jit(solution)/shard_map/ppermute | solution.py:217
  62.9 6.4 %collective-permute-start.10 = (f16[168,768]{1,0:T(8,128)(2,1)S(1)}, f16[168,768]{1,0:T(8,128)(2,1)S(1)}, u32[]{:S(2)}, u32[]{:S(2)}) collective-permute-start(f16[168,768]{1,0:T(8,128)(2,1)S(1)} %get-tuple-element.33), channel_id=1, source_target_pairs={{0,96},{1,97},{2,26},{3,27},{4,100},{5,101},{6,30},{7,31},{8,104},... | collective-permute-start | bytes 774152 | tf_op jit(solution)/shard_map/ppermute | solution.py:217
  63.0 8.1 %collective-permute-start.9 = (f16[168,768]{1,0:T(8,128)(2,1)S(1)}, f16[168,768]{1,0:T(8,128)(2,1)S(1)}, u32[]{:S(2)}, u32[]{:S(2)}) collective-permute-start(f16[168,768]{1,0:T(8,128)(2,1)S(1)} %get-tuple-element.34), channel_id=1, source_target_pairs={{0,64},{1,65},{2,18},{3,19},{4,68},{5,69},{6,22},{7,23},{8,72},{9,... | collective-permute-start | bytes 774152 | tf_op jit(solution)/shard_map/ppermute | solution.py:217
  66.4 7.5 %collective-permute-start.8 = (f16[168,768]{1,0:T(8,128)(2,1)S(1)}, f16[168,768]{1,0:T(8,128)(2,1)S(1)}, u32[]{:S(2)}, u32[]{:S(2)}) collective-permute-start(f16[168,768]{1,0:T(8,128)(2,1)S(1)} %get-tuple-element.32), channel_id=1, source_target_pairs={{0,32},{1,33},{2,10},{3,11},{4,36},{5,37},{6,14},{7,15},{8,40},{9,... | collective-permute-start | bytes 774152 | tf_op jit(solution)/shard_map/ppermute | solution.py:217
  74.5 6.6 %collective-permute-start.19 = (f16[48,384]{1,0:T(8,128)(2,1)S(1)}, f16[48,384]{1,0:T(8,128)(2,1)S(1)}, u32[]{:S(2)}, u32[]{:S(2)}) collective-permute-start(f16[48,384]{1,0:T(8,128)(2,1)S(1)} %get-tuple-element.42), channel_id=1, source_target_pairs={{0,24},{1,25},{2,26},{3,27},{4,28},{5,29},{6,30},{7,31},{8,0},{9,1... | collective-permute-start | bytes 110600 | tf_op jit(solution)/shard_map/ppermute | solution.py:217
  75.4 11.4 %collective-permute-start.14 = (f16[48,768]{1,0:T(8,128)(2,1)S(1)}, f16[48,768]{1,0:T(8,128)(2,1)S(1)}, u32[]{:S(2)}, u32[]{:S(2)}) collective-permute-start(f16[48,768]{1,0:T(8,128)(2,1)S(1)} %get-tuple-element.38), channel_id=1, source_target_pairs={{0,1},{1,4},{2,34},{3,35},{4,5},{5,0},{6,38},{7,39},{8,9},{9,12},{... | collective-permute-start | bytes 221192 | tf_op jit(solution)/shard_map/ppermute | solution.py:217
  75.4 11.3 %collective-permute-start.15 = (f16[48,768]{1,0:T(8,128)(2,1)S(1)}, f16[48,768]{1,0:T(8,128)(2,1)S(1)}, u32[]{:S(2)}, u32[]{:S(2)}) collective-permute-start(f16[48,768]{1,0:T(8,128)(2,1)S(1)} %get-tuple-element.40), channel_id=1, source_target_pairs={{0,4},{1,5},{2,66},{3,67},{4,0},{5,1},{6,70},{7,71},{8,12},{9,13},... | collective-permute-start | bytes 221192 | tf_op jit(solution)/shard_map/ppermute | solution.py:217
  76.9 9.8 %collective-permute-start.16 = (f16[48,768]{1,0:T(8,128)(2,1)S(1)}, f16[48,768]{1,0:T(8,128)(2,1)S(1)}, u32[]{:S(2)}, u32[]{:S(2)}) collective-permute-start(f16[48,768]{1,0:T(8,128)(2,1)S(1)} %get-tuple-element.39), channel_id=1, source_target_pairs={{0,5},{1,0},{2,98},{3,99},{4,1},{5,4},{6,102},{7,103},{8,13},{9,8}... | collective-permute-start | bytes 221192 | tf_op jit(solution)/shard_map/ppermute | solution.py:217
  78.6 8.0 %collective-permute-start.17 = (f16[48,384]{1,0:T(8,128)(2,1)S(1)}, f16[48,384]{1,0:T(8,128)(2,1)S(1)}, u32[]{:S(2)}, u32[]{:S(2)}) collective-permute-start(f16[48,384]{1,0:T(8,128)(2,1)S(1)} %get-tuple-element.41), channel_id=1, source_target_pairs={{0,8},{1,9},{2,10},{3,11},{4,12},{5,13},{6,14},{7,15},{8,16},{9,17... | collective-permute-start | bytes 110600 | tf_op jit(solution)/shard_map/ppermute | solution.py:217
  81.1 5.5 %collective-permute-start.18 = (f16[48,384]{1,0:T(8,128)(2,1)S(1)}, f16[48,384]{1,0:T(8,128)(2,1)S(1)}, u32[]{:S(2)}, u32[]{:S(2)}) collective-permute-start(f16[48,384]{1,0:T(8,128)(2,1)S(1)} %get-tuple-element.43), channel_id=1, source_target_pairs={{0,16},{1,17},{2,18},{3,19},{4,20},{5,21},{6,22},{7,23},{8,24},{9,... | collective-permute-start | bytes 110600 | tf_op jit(solution)/shard_map/ppermute | solution.py:217
where the time goes:
time: 88 us; the launch traced here: 87.6 us
  waiting for transfers between devices  32.7 us (37%)
  starting transfers between devices  28.7 us (33%)
  Pallas kernels  21.6 us (25%)
  other arithmetic  3.23 us (4%)
  between operations  1.07 us (1%)
    ppermute x18, waiting for transfers between devices, exchange(): lax.ppermute(chunks[k].astype(jnp.float16), AXES, routes(dims, k))  28.2 us
    ppermute x18, starting transfers between devices, exchange(): lax.ppermute(chunks[k].astype(jnp.float16), AXES, routes(dims, k))  28.1 us
    pallas_call x1, Pallas kernels, input_gradient(): pl.pallas_call(input_gradient_body, grid=(features // step,), in_specs=[p...  11.4 us
    pallas_call x4, Pallas kernels, product(): pl.pallas_call(functools.partial(product_body, step), in_specs=[pl.BlockS...  5.56 us
    ppermute x2, waiting for transfers between devices, across_cores(): return lax.ppermute(array, AXES, pairs)  4.45 us
    pallas_call x1, Pallas kernels, turn(): pl.pallas_call(turn_body, grid=(SIDE,), in_specs=[pl.BlockSpec(memory_spa...  4.06 us
  transfers between devices with their start and end apart: 20, of which 7 were waited for; matrix products, arithmetic and copies ran while one was open for 2% of the time, Pallas kernels for 16%

commit v1 on v0

v1 whole, which is shorter than its diff:
```python
import functools

import jax
import jax.numpy as jnp
from jax import lax
from jax.experimental import pallas as pl
from jax.experimental.pallas import tpu as pltpu
from jax.sharding import PartitionSpec as P


AXES = ("gx", "gy", "gz")
SIDE = 4
BLOCK = 36
PADDED = 40
TAIL = 8
LATE = (2, 1, 3)
FIRST = {"wide": "xy", "narrow": "zz"}
SECOND = {"wide": "zx", "narrow": "yy"}
THIRD = {"wide": "yz", "narrow": "xx"}
PARTS = ("wide", "narrow")
WIDE = 768
NARROW = 384


def near(array):
    return pltpu.with_memory_space_constraint(array, pltpu.VMEM)


def position(index):
    return index >> 5, index >> 3 & 3, index >> 1 & 2 | index & 1, index >> 1 & 1


def device(z, x, y, core):
    return ((z * 4 + x) * 4 + y // 2 * 2 + core) * 2 + y % 2


def routes(dims, step):
    pairs = []
    for source in range(128):
        at = dict(zip("zxyc", position(source)))
        along = dims[at["c"]]
        at[along] = (at[along] + step) % SIDE
        pairs.append((source, device(at["z"], at["x"], at["y"], at["c"])))
    return pairs


def across_cores(array):
    pairs = []
    for source in range(128):
        z, x, y, core = position(source)
        pairs.append((source, device(z, x, y, 1 - core)))
    return lax.ppermute(array, AXES, pairs)


def turned_rows(block, b, core, send, keep):
    turned = block.T
    for x in range(SIDE):
        rows = 288 * x
        piece = jnp.concatenate([turned[rows : rows + 72], turned[rows + 144 : rows + 216]], 0)

        @pl.when(core == 0)
        def _():
            keep[x, 144 * b : 144 * (b + 1)] = piece

        @pl.when(core == 1)
        def _():
            send[x, 144 * b : 144 * (b + 1)] = piece

    for y in range(SIDE):
        rows = 144 * (y // 2) + 72 + BLOCK * (y % 2)
        piece = jnp.concatenate(
            [turned[288 * x + rows : 288 * x + rows + BLOCK] for x in range(SIDE)], 0
        )

        @pl.when(core == 1)
        def _():
            keep[y, 144 * b : 144 * (b + 1)] = piece

        @pl.when(core == 0)
        def _():
            send[y, 144 * b : 144 * (b + 1)] = piece


def highest(block, top):
    most = jnp.max(jnp.abs(block), axis=0, keepdims=True)
    return most if top is None else jnp.maximum(top, most)


def turn_first_body(tokens, where, hidden, send, keep, rest, level, slots, sems):
    core = position(where[0])[3]
    width = hidden.shape[1] // SIDE
    left = hidden.shape[0] - tokens
    copies = [
        pltpu.make_async_copy(
            hidden.at[pl.ds(0, tokens), pl.ds(b * width, width)], slots.at[b], sems.at[b]
        )
        for b in range(SIDE)
    ]
    later = [
        pltpu.make_async_copy(
            hidden.at[pl.ds(tokens, left), pl.ds(b * width, width)], rest.at[b], sems.at[SIDE + b]
        )
        for b in range(SIDE)
    ]
    for copy in copies + later:
        copy.start()
    top = None
    for b, copy in enumerate(copies):
        copy.wait()
        block = slots[b]
        top = highest(block, top)
        turned_rows(block, b, core, send, keep)
    level[...] = jnp.full((TAIL, 128), jnp.max(top.astype(jnp.float32)), jnp.float32)
    for copy in later:
        copy.wait()


def turn_first(tokens, where, hidden):
    count, width = hidden.shape
    out = pltpu.VMEM((SIDE, width // 8, tokens), hidden.dtype)
    return pl.pallas_call(
        functools.partial(turn_first_body, tokens),
        in_specs=[pl.BlockSpec(memory_space=pltpu.SMEM), pl.BlockSpec(memory_space=pltpu.HBM)],
        out_specs=[pl.BlockSpec(memory_space=pltpu.VMEM)] * 4,
        out_shape=[
            out,
            out,
            pltpu.VMEM((SIDE, count - tokens, width // SIDE), hidden.dtype),
            pltpu.VMEM((TAIL, 128), jnp.float32),
        ],
        scratch_shapes=[
            pltpu.VMEM((SIDE, tokens, width // SIDE), hidden.dtype),
            pltpu.SemaphoreType.DMA((2 * SIDE,)),
        ],
        compiler_params=pltpu.CompilerParams(vmem_limit_bytes=16 * 2**20),
        cost_estimate=pl.CostEstimate(flops=10**9, bytes_accessed=4 * 10**6, transcendentals=0),
    )(where, pltpu.with_memory_space_constraint(hidden, pltpu.HBM))


def turn_rest_body(where, rest, before, send, keep, level):
    core = position(where[0])[3]
    top = None
    for b in range(SIDE):
        block = rest[b]
        top = highest(block, top)
        turned_rows(block, b, core, send, keep)
    most = jnp.maximum(before[...], jnp.max(top.astype(jnp.float32)))
    level[...] = most
    units = 144 * SIDE
    for c in range(SIDE):
        send[c, units:] = most.astype(send.dtype)


def turn_rest(where, rest, before):
    tokens, width = rest.shape[1], rest.shape[2]
    return pl.pallas_call(
        turn_rest_body,
        in_specs=[pl.BlockSpec(memory_space=pltpu.SMEM)] + [pl.BlockSpec(memory_space=pltpu.VMEM)] * 2,
        out_specs=[pl.BlockSpec(memory_space=pltpu.VMEM)] * 3,
        out_shape=[
            pltpu.VMEM((SIDE, width // 2 + TAIL, tokens), rest.dtype),
            pltpu.VMEM((SIDE, width // 2, tokens), rest.dtype),
            pltpu.VMEM((TAIL, 128), jnp.float32),
        ],
        compiler_params=pltpu.CompilerParams(vmem_limit_bytes=12 * 2**20),
        cost_estimate=pl.CostEstimate(flops=10**9, bytes_accessed=4 * 10**6, transcendentals=0),
    )(where, *map(near, (rest, before)))


def largest(values):
    return jnp.max(jnp.max(jnp.abs(values), axis=0, keepdims=True).astype(jnp.float32))


def rows_of(part, step, where, sources):
    z, x, y, core = position(where[0])
    if part == "wide":
        at = jnp.where(core == 0, x, y) + step & 3
        pieces = [source[at, 0:576] for source in sources]
    else:
        row = pl.multiple_of((z + step & 3) * 144, 16)
        pieces = [
            jnp.concatenate([source[t, pl.ds(row, 144)] for t in range(SIDE)], 0)
            for source in sources
        ]
    return jnp.concatenate(pieces, 1)


def product_body(jobs, units, grads, started, levels, where, *refs):
    refs = list(refs)
    sources = [refs.pop(0) for _ in range(units)]
    weights = [refs.pop(0) for _ in range(grads)]
    sums = [refs.pop(0) if started else None for _ in jobs]
    given = [refs.pop(0)] if levels != "bounds" else [refs.pop(0), refs.pop(0)]
    outs = [refs.pop(0) for _ in jobs]
    bits = None
    if levels == "bounds":
        top, other = given
        tokens = weights[0].shape[0]
        refs[0][0:TAIL] = top[...] * (largest(weights[0][...]) * tokens)
        refs[0][TAIL:] = jnp.full((TAIL, 128), largest(other[...]) * tokens, jnp.float32)
    elif levels == "make":
        got_top = sources[1][0, 576:].astype(jnp.float32)
        bound = given[0][0:TAIL] + given[0][TAIL:] * got_top
        bits = 15.0 - jnp.ceil(jnp.log2(jnp.maximum(bound, 2.0**-60)))
        refs[0][...] = bits
    else:
        bits = given[0][...]
    whole = weights[0][...] if grads == 1 else jnp.concatenate([w[...] for w in weights], 0)
    for (part, step), before, out in zip(jobs, sums, outs):
        left = rows_of(part, step, where, sources)
        columns = whole[:, :WIDE] if part == "wide" else whole[:, WIDE:]
        value = jnp.dot(left, columns, preferred_element_type=jnp.float32)
        if before is not None:
            value = before[...] + value
        if levels == "bounds" or step == 0:
            out[0:576] = value
        else:
            out[0:576] = value * jnp.exp2(bits)[0:1, 0:1]
            out[576:] = jnp.broadcast_to(bits[:, 0:1], (TAIL, out.shape[1]))


def product(jobs, where, sources, weights, levels, given, sums=()):
    tail = 0 if levels == "bounds" else TAIL
    outs = [
        pltpu.VMEM((576 + (tail if step else 0), WIDE if part == "wide" else NARROW), jnp.float32)
        for part, step in jobs
    ]
    if levels == "bounds":
        outs.append(pltpu.VMEM((2 * TAIL, 128), jnp.float32))
    elif levels == "make":
        outs.append(pltpu.VMEM((TAIL, 128), jnp.float32))
    inputs = [*sources, *weights, *sums, *given]
    tokens = sum(source.shape[2] for source in sources)
    flops = sum(2 * 576 * tokens * (WIDE if part == "wide" else NARROW) for part, _ in jobs)
    return pl.pallas_call(
        functools.partial(product_body, jobs, len(sources), len(weights), bool(sums), levels),
        in_specs=[pl.BlockSpec(memory_space=pltpu.SMEM)]
        + [pl.BlockSpec(memory_space=pltpu.VMEM)] * len(inputs),
        out_specs=[pl.BlockSpec(memory_space=pltpu.VMEM)] * len(outs),
        out_shape=outs,
        compiler_params=pltpu.CompilerParams(vmem_limit_bytes=12 * 2**20),
        cost_estimate=pl.CostEstimate(flops=flops, bytes_accessed=10**6, transcendentals=0),
    )(where, *map(near, inputs))


def power(part, rows):
    return jnp.exp2(-part[rows : rows + 1].astype(jnp.float32))


def total(own, parts, rows):
    value = own[0:rows]
    for part in parts:
        value = value + part[0:rows].astype(jnp.float32) * power(part, rows)
    return value


def spread_body(part, high, blocks, where, value, tails, before, *refs):
    z, x, y, core = position(where[0])
    swap = core == (0 if part == "wide" else 1)
    if blocks == 16:
        at = jnp.where(swap, z, x) if part == "wide" else y
        major, minor = jnp.where(swap, 4, 1), jnp.where(swap, 1, 4)
    else:
        at = jnp.where(swap, y, z) if part == "wide" else x
        major, minor = 1, 0
    outs, level, scratch = refs[0:4], refs[4], refs[5]
    width = value.shape[1]
    bits = jnp.minimum(jnp.min(tails[...], axis=0, keepdims=True), before[0:1]) - 2.0
    level[...] = jnp.broadcast_to(bits, (TAIL, 128))
    scale = jnp.exp2(bits)[0:1, 0:1]
    for i in range(blocks):
        scratch[i, 0:BLOCK] = value[BLOCK * i : BLOCK * (i + 1)]
    for k in range(SIDE):
        chunk = at + k & 3
        for t in range(blocks // SIDE):
            piece = scratch[chunk * major + t * minor, 0:BLOCK]
            outs[k][BLOCK * t : BLOCK * (t + 1)] = piece * scale if k else piece
        end = BLOCK * blocks // SIDE
        if high > end:
            outs[k][end:high] = jnp.zeros((high - end, width), jnp.float32)
        if k:
            outs[k][high:] = jnp.broadcast_to(bits[:, 0:1], (TAIL, width))


def spread(where, part, blocks, own, parts, own_bits):
    rows = BLOCK * blocks
    kept = -(-rows // SIDE // TAIL) * TAIL
    width = own.shape[1]
    tails = [piece[rows:, 0:128].astype(jnp.float32) for piece in parts]
    inputs = [total(own, parts, rows), jnp.concatenate(tails, 0), own_bits]
    out = pl.pallas_call(
        functools.partial(spread_body, part, kept, blocks),
        in_specs=[pl.BlockSpec(memory_space=pltpu.SMEM)] + [pl.BlockSpec(memory_space=pltpu.VMEM)] * 3,
        out_specs=[pl.BlockSpec(memory_space=pltpu.VMEM)] * 5,
        out_shape=[pltpu.VMEM((kept, width), jnp.float32)]
        + [pltpu.VMEM((kept + TAIL, width), jnp.float32)] * 3
        + [pltpu.VMEM((TAIL, 128), jnp.float32)],
        scratch_shapes=[pltpu.VMEM((blocks, PADDED, width), jnp.float32)],
        compiler_params=pltpu.CompilerParams(vmem_limit_bytes=12 * 2**20),
        cost_estimate=pl.CostEstimate(flops=10**8, bytes_accessed=10**7, transcendentals=0),
    )(where, *map(near, inputs))
    return out[:4], out[4]


def exchange(chunks, dims):
    arrived = {}
    for k in chunks:
        arrived[k] = lax.ppermute(chunks[k].astype(jnp.float16), AXES, routes(dims, k))
    return arrived


def input_gradient_body(grad, weight, out, loads, stores, load_sems, store_sems):
    count, step = loads.shape[0], loads.shape[1]
    incoming = [
        pltpu.make_async_copy(weight.at[pl.ds(i * step, step)], loads.at[i], load_sems.at[i])
        for i in range(count)
    ]
    outgoing = [
        pltpu.make_async_copy(stores.at[i], out.at[:, pl.ds(i * step, step)], store_sems.at[i])
        for i in range(count)
    ]
    for copy in incoming:
        copy.start()
    for i in range(count):
        incoming[i].wait()
        stores[i] = lax.dot_general(
            grad[...], loads[i], (((1,), (1,)), ((), ())), preferred_element_type=jnp.float32
        ).astype(out.dtype)
        outgoing[i].start()
    for copy in outgoing:
        copy.wait()


def input_gradient(grad, weight):
    tokens, width = grad.shape
    features = weight.shape[0]
    count = 9
    return pl.pallas_call(
        input_gradient_body,
        in_specs=[pl.BlockSpec(memory_space=pltpu.VMEM), pl.BlockSpec(memory_space=pltpu.HBM)],
        out_specs=pl.BlockSpec(memory_space=pltpu.HBM),
        out_shape=pltpu.HBM((tokens, features), grad.dtype),
        scratch_shapes=[
            pltpu.VMEM((count, features // count, width), weight.dtype),
            pltpu.VMEM((count, tokens, features // count), grad.dtype),
            pltpu.SemaphoreType.DMA((count,)),
            pltpu.SemaphoreType.DMA((count,)),
        ],
        compiler_params=pltpu.CompilerParams(vmem_limit_bytes=18 * 2**20),
        cost_estimate=pl.CostEstimate(
            flops=2 * tokens * width * features, bytes_accessed=15 * 10**6, transcendentals=0
        ),
    )(near(grad), pltpu.with_memory_space_constraint(weight, pltpu.HBM))


def listed(parts):
    return [parts[k] for k in (1, 2, 3)]


def body(hidden, out_grad, down_weight):
    where = lax.axis_index(AXES).reshape(1)
    tokens = hidden.shape[0] * 128
    factor = 1.0 / float(tokens) ** 0.5

    other_grad = across_cores(out_grad)
    send_one, keep_one, rest, top = turn_first(256, where, hidden)
    got_one = across_cores(send_one)
    send_two, keep_two, top = turn_rest(where, rest, top)
    got_two = across_cores(send_two)
    kept, got = (keep_one, keep_two), (got_one, got_two)

    early = (("wide", 1), ("wide", 3), ("narrow", 1), ("narrow", 3))
    *sums, bounds = product(early, where, kept, [out_grad], "bounds", [top, other_grad])
    arrived = {"wide": {}, "narrow": {}}
    level = None
    for jobs, started in ((early[:1], sums[:1]), (early[1:2], sums[1:2]), (early[2:], sums[2:])):
        if level is None:
            value, level = product(jobs, where, got, [other_grad], "make", [bounds], started)
            values = [value]
        else:
            values = product(jobs, where, got, [other_grad], "use", [level], started)
        for (part, k), value in zip(jobs, values):
            arrived[part] |= exchange({k: value}, FIRST[part])
    both, grads = (*kept, *got), [out_grad, other_grad]
    jobs = (("wide", 2), ("narrow", 2))
    values = product(jobs, where, both, grads, "use", [level])
    for (part, k), value in zip(jobs, values):
        arrived[part] |= exchange({k: value}, FIRST[part])

    hidden_grad = input_gradient(out_grad, down_weight)
    stay = product((("wide", 0), ("narrow", 0)), where, both, grads, "use", [level])

    columns = []
    for part, own in zip(PARTS, stay):
        (own, *chunks), bits = spread(where, part, 16, own, listed(arrived[part]), level)
        parts = exchange({k: chunks[k - 1] for k in LATE}, SECOND[part])
        (own, *chunks), bits = spread(where, part, 4, own, listed(parts), bits)
        parts = exchange({k: chunks[k - 1] for k in LATE}, THIRD[part])
        columns.append(total(own, listed(parts), PADDED)[0:BLOCK])
    weight_grad = jnp.concatenate(columns, 1) * factor
    return (weight_grad, hidden_grad)


def solution(mesh):
    in_specs = (P(AXES, None), P(AXES, None), P())
    out_specs = (P(AXES, None), P(AXES, None))
    return jax.shard_map(body, mesh=mesh, in_specs=in_specs, out_specs=out_specs, check_vma=False)
```

time: 88 us -> 87.2 us (level)
  the two profiles are of different devices: /device:TPU:6 before, /device:TPU:0 now
where the time goes in v1:
time: 87.2 us; the launch traced here: 87.1 us
  starting transfers between devices  34.7 us (40%)
  waiting for transfers between devices  27.8 us (32%)
  Pallas kernels  20.3 us (23%)
  other arithmetic  3.05 us (3%)
  between operations  1.08 us (1%)
    ppermute x18, starting transfers between devices, exchange(): lax.ppermute(chunks[k].astype(jnp.float16), AXES, routes(dims, k))  34 us
    ppermute x18, waiting for transfers between devices, exchange(): lax.ppermute(chunks[k].astype(jnp.float16), AXES, routes(dims, k))  25.4 us
    pallas_call x1, Pallas kernels, input_gradient(): pl.pallas_call(input_gradient_body, in_specs=[pl.BlockSpec(memory_space=p...  8.54 us
    pallas_call x6, Pallas kernels, product(): pl.pallas_call(functools.partial(product_body, jobs, len(sources), len(we...  6.58 us
    pallas_call x1, Pallas kernels, turn_first(): pl.pallas_call(functools.partial(turn_first_body, tokens), in_specs=[pl.B...  2.5 us
    ppermute x3, waiting for transfers between devices, across_cores(): return lax.ppermute(array, AXES, pairs)  2.43 us
  transfers between devices with their start and end apart: 21, of which 10 were waited for; matrix products, arithmetic and copies ran while one was open for 2% of the time, Pallas kernels for 17%

profile of v1, /device:TPU:0, one launch (start us, length us, event | category | flops | bytes accessed | tf_op | source)
XLA Modules:
  0.0 87.1 jit_solution(11657043863848055736)
XLA Ops:
  0.6 2.5 %shard_map.50 = (bf16[4,576,256]{2,1,0:T(8,128)(2,1)S(1)}, bf16[4,576,256]{2,1,0:T(8,128)(2,1)S(1)}, bf16[4,128,1152]{2,1,0:T(8,128)(2,1)S(1)}, f32[8,128]{1,0:T(8,128)S(1)}) custom-call(s32[1]{0:T(128)} %bitcast.where, bf16[384,4608]{1,0:T(8,128)(2,1)} %hidden.1), custom_call_target="tpu_custom_call" | custom-call | flops 1000000000 | bytes 4000000 | tf_op jit(solution)/shard_map/pallas_call | solution.py:121
  3.8 0.9 %shard_map.51 = (bf16[4,584,128]{2,1,0:T(8,128)(2,1)S(1)}, bf16[4,576,128]{2,1,0:T(8,128)(2,1)S(1)}, f32[8,128]{1,0:T(8,128)S(1)}) custom-call(s32[1]{0:T(128)} %bitcast.where, bf16[4,128,1152]{2,1,0:T(8,128)(2,1)S(1)} %get-tuple-element.41.rest, f32[8,128]{1,0:T(8,128)S(1)} %get-tuple-element.42.before), custom_call_target="tpu_custom_call" | custom-call | flops 1000000000 | bytes 4000000 | tf_op jit(solution)/shard_map/pallas_call | solution.py:156
  4.9 2.4 %collective-permute-done.2.refs_4_.refs_2_.refs_5_ = bf16[384,1152]{1,0:T(8,128)(2,1)S(1)} collective-permute-done((bf16[384,1152]{1,0:T(8,128)(2,1)S(1)}, bf16[384,1152]{1,0:T(8,128)(2,1)S(1)}, u32[]{:S(2)}, u32[]{:S(2)}) %collective-permute-start.2) | collective-permute-done | bytes 884768 | tf_op jit(solution)/shard_map/ppermute | solution.py:52
  7.4 1.9 %shard_map.52 = (f32[576,768]{1,0:T(8,128)S(1)}, f32[576,768]{1,0:T(8,128)S(1)}, f32[576,384]{1,0:T(8,128)S(1)}, f32[576,384]{1,0:T(8,128)S(1)}, f32[16,128]{1,0:T(8,128)S(1)}) custom-call(s32[1]{0:T(128)} %bitcast.where, bf16[4,576,256]{2,1,0:T(8,128)(2,1)S(1)} %get-tuple-element.40.refs_0_, bf16[4,576,128]{2,1,0:T(8,128)(2,1)S(1)} %get-tuple-element.43.refs_1_, ...), custom_call_target="tpu_custom_call" | custom-call | flops 1019215872 | bytes 1000000 | tf_op jit(solution)/shard_map/pallas_call | solution.py:235
  9.9 1.3 %shard_map.55 = (f32[584,768]{1,0:T(8,128)S(1)}, f32[584,384]{1,0:T(8,128)S(1)}) custom-call(s32[1]{0:T(128)} %bitcast.where, bf16[4,576,256]{2,1,0:T(8,128)(2,1)S(1)} %get-tuple-element.40.refs_0_, bf16[4,576,128]{2,1,0:T(8,128)(2,1)S(1)} %get-tuple-element.43.refs_1_, bf16[4,576,256]{2,1,0:T(8,128)(2,1)S(1)} %collective-permute-done.refs_0_.refs_2_, ...), custom_call_target="tpu_custom_call" | custom-call | flops 1019215872 | bytes 1000000 | tf_op jit(solution)/shard_map/pallas_call | solution.py:235
  11.3 4.1 %collective-permute-start.13 = (f16[584,384]{1,0:T(8,128)(2,1)S(1)}, f16[584,384]{1,0:T(8,128)(2,1)S(1)}, u32[]{:S(2)}, u32[]{:S(2)}) collective-permute-start(f16[584,384]{1,0:T(8,128)(2,1)S(1)} %convert_element_type.204), channel_id=1, source_target_pairs={{0,64},{1,65},{2,66},{3,67},{4,68},{5,69},{6,70},{7,71},{8,72},{9,... | collective-permute-start | bytes 1345544 | tf_op jit(solution)/shard_map/ppermute | solution.py:308
  15.4 0.7 shard_map.59
  16.2 1.1 %collective-permute-start.12 = (f16[584,384]{1,0:T(8,128)(2,1)S(1)}, f16[584,384]{1,0:T(8,128)(2,1)S(1)}, u32[]{:S(2)}, u32[]{:S(2)}) collective-permute-start(f16[584,384]{1,0:T(8,128)(2,1)S(1)} %convert_element_type.201), channel_id=1, source_target_pairs={{0,32},{1,33},{2,34},{3,35},{4,36},{5,37},{6,38},{7,39},{8,40},{9,... | collective-permute-start | bytes 1345544 | tf_op jit(solution)/shard_map/ppermute | solution.py:308
  17.4 2.3 %collective-permute-start.14 = (f16[584,384]{1,0:T(8,128)(2,1)S(1)}, f16[584,384]{1,0:T(8,128)(2,1)S(1)}, u32[]{:S(2)}, u32[]{:S(2)}) collective-permute-start(f16[584,384]{1,0:T(8,128)(2,1)S(1)} %convert_element_type.207), channel_id=1, source_target_pairs={{0,96},{1,97},{2,98},{3,99},{4,100},{5,101},{6,102},{7,103},{8,104... | collective-permute-start | bytes 1345544 | tf_op jit(solution)/shard_map/ppermute | solution.py:308
  20.4 2.8 %collective-permute-start.5 = (f16[584,768]{1,0:T(8,128)(2,1)S(1)}, f16[584,768]{1,0:T(8,128)(2,1)S(1)}, u32[]{:S(2)}, u32[]{:S(2)}) collective-permute-start(f16[584,768]{1,0:T(8,128)(2,1)S(1)} %convert_element_type.180), channel_id=1, source_target_pairs={{0,24},{1,25},{2,7},{3,2},{4,28},{5,29},{6,3},{7,6},{8,0},{9,1},{1... | collective-permute-start | bytes 2691080 | tf_op jit(solution)/shard_map/ppermute | solution.py:308
  23.4 0.9 %collective-permute-start.4 = (f16[584,768]{1,0:T(8,128)(2,1)S(1)}, f16[584,768]{1,0:T(8,128)(2,1)S(1)}, u32[]{:S(2)}, u32[]{:S(2)}) collective-permute-start(f16[584,768]{1,0:T(8,128)(2,1)S(1)} %convert_element_type.177), channel_id=1, source_target_pairs={{0,16},{1,17},{2,6},{3,7},{4,20},{5,21},{6,2},{7,3},{8,24},{9,25},... | collective-permute-start | bytes 2691080 | tf_op jit(solution)/shard_map/ppermute | solution.py:308
  24.2 1.3 %shard_map.54 = (f32[576,768]{1,0:T(8,128)S(1)}, f32[576,384]{1,0:T(8,128)S(1)}) custom-call(s32[1]{0:T(128)} %bitcast.where, bf16[4,576,256]{2,1,0:T(8,128)(2,1)S(1)} %get-tuple-element.40.refs_0_, bf16[4,576,128]{2,1,0:T(8,128)(2,1)S(1)} %get-tuple-element.43.refs_1_, bf16[4,576,256]{2,1,0:T(8,128)(2,1)S(1)} %collective-permute-done.refs_0_.refs_2_, ...), custom_call_target="tpu_custom_call" | custom-call | flops 1019215872 | bytes 1000000 | tf_op jit(solution)/shard_map/pallas_call | solution.py:235
  25.6 1.0 %collective-permute-done.13 = f16[584,384]{1,0:T(8,128)(2,1)S(1)} collective-permute-done((f16[584,384]{1,0:T(8,128)(2,1)S(1)}, f16[584,384]{1,0:T(8,128)(2,1)S(1)}, u32[]{:S(2)}, u32[]{:S(2)}) %collective-permute-start.13) | collective-permute-done | bytes 448544 | tf_op jit(solution)/shard_map/ppermute | solution.py:308
  26.6 9.0 %collective-permute-done.12 = f16[584,384]{1,0:T(8,128)(2,1)S(1)} collective-permute-done((f16[584,384]{1,0:T(8,128)(2,1)S(1)}, f16[584,384]{1,0:T(8,128)(2,1)S(1)}, u32[]{:S(2)}, u32[]{:S(2)}) %collective-permute-start.12) | collective-permute-done | bytes 448544 | tf_op jit(solution)/shard_map/ppermute | solution.py:308
  35.6 0.8 collective-permute-done.14
  37.0 1.7 %collective-permute-start.15 = (f16[152,384]{1,0:T(8,128)(2,1)S(1)}, f16[152,384]{1,0:T(8,128)(2,1)S(1)}, u32[]{:S(2)}, u32[]{:S(2)}) collective-permute-start(f16[152,384]{1,0:T(8,128)(2,1)S(1)} %convert_element_type.210), channel_id=1, source_target_pairs={{0,1},{1,4},{2,3},{3,6},{4,5},{5,0},{6,7},{7,2},{8,9},{9,12},{10,1... | collective-permute-start | bytes 350216 | tf_op jit(solution)/shard_map/ppermute | solution.py:308
  38.7 3.0 %collective-permute-start.16 = (f16[152,384]{1,0:T(8,128)(2,1)S(1)}, f16[152,384]{1,0:T(8,128)(2,1)S(1)}, u32[]{:S(2)}, u32[]{:S(2)}) collective-permute-start(f16[152,384]{1,0:T(8,128)(2,1)S(1)} %convert_element_type.213), channel_id=1, source_target_pairs={{0,4},{1,5},{2,6},{3,7},{4,0},{5,1},{6,2},{7,3},{8,12},{9,13},{10,... | collective-permute-start | bytes 350216 | tf_op jit(solution)/shard_map/ppermute | solution.py:308
  41.6 1.6 %collective-permute-start.17 = (f16[152,384]{1,0:T(8,128)(2,1)S(1)}, f16[152,384]{1,0:T(8,128)(2,1)S(1)}, u32[]{:S(2)}, u32[]{:S(2)}) collective-permute-start(f16[152,384]{1,0:T(8,128)(2,1)S(1)} %convert_element_type.216), channel_id=1, source_target_pairs={{0,5},{1,0},{2,7},{3,2},{4,1},{5,4},{6,3},{7,6},{8,13},{9,8},{10,1... | collective-permute-start | bytes 350216 | tf_op jit(solution)/shard_map/ppermute | solution.py:308
  43.3 8.5 %shard_map.62 = bf16[384,4608]{1,0:T(8,128)(2,1)} custom-call(bf16[384,1152]{1,0:T(8,128)(2,1)S(1)} %copy-done, bf16[4608,1152]{1,0:T(8,128)(2,1)} %weight.1), custom_call_target="tpu_custom_call" | custom-call | flops 4076863488 | bytes 15000000 | tf_op jit(solution)/shard_map/pallas_call | solution.py:338
  51.9 1.6 %collective-permute-start.3 = (f16[584,768]{1,0:T(8,128)(2,1)S(1)}, f16[584,768]{1,0:T(8,128)(2,1)S(1)}, u32[]{:S(2)}, u32[]{:S(2)}) collective-permute-start(f16[584,768]{1,0:T(8,128)(2,1)S(1)} %convert_element_type.174), channel_id=1, source_target_pairs={{0,8},{1,9},{2,3},{3,6},{4,12},{5,13},{6,7},{7,2},{8,16},{9,17},{1... | collective-permute-start | bytes 2691080 | tf_op jit(solution)/shard_map/ppermute | solution.py:308
  54.3 1.6 %collective-permute-start.18 = (f16[48,384]{1,0:T(8,128)(2,1)S(1)}, f16[48,384]{1,0:T(8,128)(2,1)S(1)}, u32[]{:S(2)}, u32[]{:S(2)}) collective-permute-start(f16[48,384]{1,0:T(8,128)(2,1)S(1)} %convert_element_type.219), channel_id=1, source_target_pairs={{0,8},{1,9},{2,10},{3,11},{4,12},{5,13},{6,14},{7,15},{8,16},{9,17... | collective-permute-start | bytes 110600 | tf_op jit(solution)/shard_map/ppermute | solution.py:308
  55.9 1.8 %collective-permute-start.19 = (f16[48,384]{1,0:T(8,128)(2,1)S(1)}, f16[48,384]{1,0:T(8,128)(2,1)S(1)}, u32[]{:S(2)}, u32[]{:S(2)}) collective-permute-start(f16[48,384]{1,0:T(8,128)(2,1)S(1)} %convert_element_type.222), channel_id=1, source_target_pairs={{0,16},{1,17},{2,18},{3,19},{4,20},{5,21},{6,22},{7,23},{8,24},{9,... | collective-permute-start | bytes 110600 | tf_op jit(solution)/shard_map/ppermute | solution.py:308
  57.7 2.2 %collective-permute-start.20 = (f16[48,384]{1,0:T(8,128)(2,1)S(1)}, f16[48,384]{1,0:T(8,128)(2,1)S(1)}, u32[]{:S(2)}, u32[]{:S(2)}) collective-permute-start(f16[48,384]{1,0:T(8,128)(2,1)S(1)} %convert_element_type.225), channel_id=1, source_target_pairs={{0,24},{1,25},{2,26},{3,27},{4,28},{5,29},{6,30},{7,31},{8,0},{9,1... | collective-permute-start | bytes 110600 | tf_op jit(solution)/shard_map/ppermute | solution.py:308
  60.0 6.8 %collective-permute-done.3 = f16[584,768]{1,0:T(8,128)(2,1)S(1)} collective-permute-done((f16[584,768]{1,0:T(8,128)(2,1)S(1)}, f16[584,768]{1,0:T(8,128)(2,1)S(1)}, u32[]{:S(2)}, u32[]{:S(2)}) %collective-permute-start.3) | collective-permute-done | bytes 897056 | tf_op jit(solution)/shard_map/ppermute | solution.py:308
  67.8 1.1 %collective-permute-start.6 = (f16[152,768]{1,0:T(8,128)(2,1)S(1)}, f16[152,768]{1,0:T(8,128)(2,1)S(1)}, u32[]{:S(2)}, u32[]{:S(2)}) collective-permute-start(f16[152,768]{1,0:T(8,128)(2,1)S(1)} %convert_element_type.183), channel_id=1, source_target_pairs={{0,32},{1,33},{2,10},{3,11},{4,36},{5,37},{6,14},{7,15},{8,40},{9,... | collective-permute-start | bytes 700424 | tf_op jit(solution)/shard_map/ppermute | solution.py:308
  68.9 3.2 %collective-permute-start.7 = (f16[152,768]{1,0:T(8,128)(2,1)S(1)}, f16[152,768]{1,0:T(8,128)(2,1)S(1)}, u32[]{:S(2)}, u32[]{:S(2)}) collective-permute-start(f16[152,768]{1,0:T(8,128)(2,1)S(1)} %convert_element_type.186), channel_id=1, source_target_pairs={{0,64},{1,65},{2,18},{3,19},{4,68},{5,69},{6,22},{7,23},{8,72},{9,... | collective-permute-start | bytes 700424 | tf_op jit(solution)/shard_map/ppermute | solution.py:308
  72.1 1.1 %collective-permute-start.8 = (f16[152,768]{1,0:T(8,128)(2,1)S(1)}, f16[152,768]{1,0:T(8,128)(2,1)S(1)}, u32[]{:S(2)}, u32[]{:S(2)}) collective-permute-start(f16[152,768]{1,0:T(8,128)(2,1)S(1)} %convert_element_type.189), channel_id=1, source_target_pairs={{0,96},{1,97},{2,26},{3,27},{4,100},{5,101},{6,30},{7,31},{8,104},... | collective-permute-start | bytes 700424 | tf_op jit(solution)/shard_map/ppermute | solution.py:308
  73.4 1.8 %collective-permute-done.6 = f16[152,768]{1,0:T(8,128)(2,1)S(1)} collective-permute-done((f16[152,768]{1,0:T(8,128)(2,1)S(1)}, f16[152,768]{1,0:T(8,128)(2,1)S(1)}, u32[]{:S(2)}, u32[]{:S(2)}) %collective-permute-start.6) | collective-permute-done | bytes 233504 | tf_op jit(solution)/shard_map/ppermute | solution.py:308
  75.2 3.4 %collective-permute-done.7 = f16[152,768]{1,0:T(8,128)(2,1)S(1)} collective-permute-done((f16[152,768]{1,0:T(8,128)(2,1)S(1)}, f16[152,768]{1,0:T(8,128)(2,1)S(1)}, u32[]{:S(2)}, u32[]{:S(2)}) %collective-permute-start.7) | collective-permute-done | bytes 233504 | tf_op jit(solution)/shard_map/ppermute | solution.py:308
  81.0 2.7 %collective-permute-start.11 = (f16[48,768]{1,0:T(8,128)(2,1)S(1)}, f16[48,768]{1,0:T(8,128)(2,1)S(1)}, u32[]{:S(2)}, u32[]{:S(2)}) collective-permute-start(f16[48,768]{1,0:T(8,128)(2,1)S(1)} %convert_element_type.198), channel_id=1, source_target_pairs={{0,5},{1,0},{2,98},{3,99},{4,1},{5,4},{6,102},{7,103},{8,13},{9,8}... | collective-permute-start | bytes 221192 | tf_op jit(solution)/shard_map/ppermute | solution.py:308
  83.7 1.8 %collective-permute-done.10 = f16[48,768]{1,0:T(8,128)(2,1)S(1)} collective-permute-done((f16[48,768]{1,0:T(8,128)(2,1)S(1)}, f16[48,768]{1,0:T(8,128)(2,1)S(1)}, u32[]{:S(2)}, u32[]{:S(2)}) %collective-permute-start.10) | collective-permute-done | bytes 73760 | tf_op jit(solution)/shard_map/ppermute | solution.py:308
  85.5 0.7 collective-permute-done.9
  (90 shorter events, 8.5 us)
Async XLA Ops:
  0.6 2.6 %copy-start = (bf16[384,1152]{1,0:T(8,128)(2,1)S(1)}, bf16[384,1152]{1,0:T(8,128)(2,1)}, u32[]{:S(2)}) copy-start(bf16[384,1152]{1,0:T(8,128)(2,1)} %grad.1) | copy-start | bytes 2654212
  3.2 6.1 %collective-permute-start = (bf16[4,576,256]{2,1,0:T(8,128)(2,1)S(1)}, bf16[4,576,256]{2,1,0:T(8,128)(2,1)S(1)}, u32[]{:S(2)}, u32[]{:S(2)}) collective-permute-start(bf16[4,576,256]{2,1,0:T(8,128)(2,1)S(1)} %get-tuple-element.44), channel_id=1, source_target_pairs={{0,2},{1,3},{2,0},{3,1},{4,6},{5,7},{6,4},{7,5},{8,10},{9,11},{10,... | collective-permute-start | bytes 3538952 | tf_op jit(solution)/shard_map/ppermute | solution.py:52
  3.3 4.1 %collective-permute-start.2 = (bf16[384,1152]{1,0:T(8,128)(2,1)S(1)}, bf16[384,1152]{1,0:T(8,128)(2,1)S(1)}, u32[]{:S(2)}, u32[]{:S(2)}) collective-permute-start(bf16[384,1152]{1,0:T(8,128)(2,1)S(1)} %copy-done), channel_id=1, source_target_pairs={{0,2},{1,3},{2,0},{3,1},{4,6},{5,7},{6,4},{7,5},{8,10},{9,11},{10,... | collective-permute-start | bytes 2654216 | tf_op jit(solution)/shard_map/ppermute | solution.py:52
  4.7 4.6 %collective-permute-start.1 = (bf16[4,584,128]{2,1,0:T(8,128)(2,1)S(1)}, bf16[4,584,128]{2,1,0:T(8,128)(2,1)S(1)}, u32[]{:S(2)}, u32[]{:S(2)}) collective-permute-start(bf16[4,584,128]{2,1,0:T(8,128)(2,1)S(1)} %get-tuple-element.45), channel_id=1, source_target_pairs={{0,2},{1,3},{2,0},{3,1},{4,6},{5,7},{6,4},{7,5},{8,10},{9,11},{10,... | collective-permute-start | bytes 1794056 | tf_op jit(solution)/shard_map/ppermute | solution.py:52
  11.3 15.3 %collective-permute-start.13 = (f16[584,384]{1,0:T(8,128)(2,1)S(1)}, f16[584,384]{1,0:T(8,128)(2,1)S(1)}, u32[]{:S(2)}, u32[]{:S(2)}) collective-permute-start(f16[584,384]{1,0:T(8,128)(2,1)S(1)} %convert_element_type.204), channel_id=1, source_target_pairs={{0,64},{1,65},{2,66},{3,67},{4,68},{5,69},{6,70},{7,71},{8,72},{9,... | collective-permute-start | bytes 1345544 | tf_op jit(solution)/shard_map/ppermute | solution.py:308
  16.2 19.4 %collective-permute-start.12 = (f16[584,384]{1,0:T(8,128)(2,1)S(1)}, f16[584,384]{1,0:T(8,128)(2,1)S(1)}, u32[]{:S(2)}, u32[]{:S(2)}) collective-permute-start(f16[584,384]{1,0:T(8,128)(2,1)S(1)} %convert_element_type.201), channel_id=1, source_target_pairs={{0,32},{1,33},{2,34},{3,35},{4,36},{5,37},{6,38},{7,39},{8,40},{9,... | collective-permute-start | bytes 1345544 | tf_op jit(solution)/shard_map/ppermute | solution.py:308
  17.4 19.0 %collective-permute-start.14 = (f16[584,384]{1,0:T(8,128)(2,1)S(1)}, f16[584,384]{1,0:T(8,128)(2,1)S(1)}, u32[]{:S(2)}, u32[]{:S(2)}) collective-permute-start(f16[584,384]{1,0:T(8,128)(2,1)S(1)} %convert_element_type.207), channel_id=1, source_target_pairs={{0,96},{1,97},{2,98},{3,99},{4,100},{5,101},{6,102},{7,103},{8,104... | collective-permute-start | bytes 1345544 | tf_op jit(solution)/shard_map/ppermute | solution.py:308
  20.4 37.3 %collective-permute-start.5 = (f16[584,768]{1,0:T(8,128)(2,1)S(1)}, f16[584,768]{1,0:T(8,128)(2,1)S(1)}, u32[]{:S(2)}, u32[]{:S(2)}) collective-permute-start(f16[584,768]{1,0:T(8,128)(2,1)S(1)} %convert_element_type.180), channel_id=1, source_target_pairs={{0,24},{1,25},{2,7},{3,2},{4,28},{5,29},{6,3},{7,6},{8,0},{9,1},{1... | collective-permute-start | bytes 2691080 | tf_op jit(solution)/shard_map/ppermute | solution.py:308
  23.4 36.6 %collective-permute-start.4 = (f16[584,768]{1,0:T(8,128)(2,1)S(1)}, f16[584,768]{1,0:T(8,128)(2,1)S(1)}, u32[]{:S(2)}, u32[]{:S(2)}) collective-permute-start(f16[584,768]{1,0:T(8,128)(2,1)S(1)} %convert_element_type.177), channel_id=1, source_target_pairs={{0,16},{1,17},{2,6},{3,7},{4,20},{5,21},{6,2},{7,3},{8,24},{9,25},... | collective-permute-start | bytes 2691080 | tf_op jit(solution)/shard_map/ppermute | solution.py:308
  37.0 14.9 %collective-permute-start.15 = (f16[152,384]{1,0:T(8,128)(2,1)S(1)}, f16[152,384]{1,0:T(8,128)(2,1)S(1)}, u32[]{:S(2)}, u32[]{:S(2)}) collective-permute-start(f16[152,384]{1,0:T(8,128)(2,1)S(1)} %convert_element_type.210), channel_id=1, source_target_pairs={{0,1},{1,4},{2,3},{3,6},{4,5},{5,0},{6,7},{7,2},{8,9},{9,12},{10,1... | collective-permute-start | bytes 350216 | tf_op jit(solution)/shard_map/ppermute | solution.py:308
  38.7 14.9 %collective-permute-start.16 = (f16[152,384]{1,0:T(8,128)(2,1)S(1)}, f16[152,384]{1,0:T(8,128)(2,1)S(1)}, u32[]{:S(2)}, u32[]{:S(2)}) collective-permute-start(f16[152,384]{1,0:T(8,128)(2,1)S(1)} %convert_element_type.213), channel_id=1, source_target_pairs={{0,4},{1,5},{2,6},{3,7},{4,0},{5,1},{6,2},{7,3},{8,12},{9,13},{10,... | collective-permute-start | bytes 350216 | tf_op jit(solution)/shard_map/ppermute | solution.py:308
  41.6 11.9 %collective-permute-start.17 = (f16[152,384]{1,0:T(8,128)(2,1)S(1)}, f16[152,384]{1,0:T(8,128)(2,1)S(1)}, u32[]{:S(2)}, u32[]{:S(2)}) collective-permute-start(f16[152,384]{1,0:T(8,128)(2,1)S(1)} %convert_element_type.216), channel_id=1, source_target_pairs={{0,5},{1,0},{2,7},{3,2},{4,1},{5,4},{6,3},{7,6},{8,13},{9,8},{10,1... | collective-permute-start | bytes 350216 | tf_op jit(solution)/shard_map/ppermute | solution.py:308
  51.9 14.8 %collective-permute-start.3 = (f16[584,768]{1,0:T(8,128)(2,1)S(1)}, f16[584,768]{1,0:T(8,128)(2,1)S(1)}, u32[]{:S(2)}, u32[]{:S(2)}) collective-permute-start(f16[584,768]{1,0:T(8,128)(2,1)S(1)} %convert_element_type.174), channel_id=1, source_target_pairs={{0,8},{1,9},{2,3},{3,6},{4,12},{5,13},{6,7},{7,2},{8,16},{9,17},{1... | collective-permute-start | bytes 2691080 | tf_op jit(solution)/shard_map/ppermute | solution.py:308
  54.3 18.9 %collective-permute-start.18 = (f16[48,384]{1,0:T(8,128)(2,1)S(1)}, f16[48,384]{1,0:T(8,128)(2,1)S(1)}, u32[]{:S(2)}, u32[]{:S(2)}) collective-permute-start(f16[48,384]{1,0:T(8,128)(2,1)S(1)} %convert_element_type.219), channel_id=1, source_target_pairs={{0,8},{1,9},{2,10},{3,11},{4,12},{5,13},{6,14},{7,15},{8,16},{9,17... | collective-permute-start | bytes 110600 | tf_op jit(solution)/shard_map/ppermute | solution.py:308
  55.9 17.4 %collective-permute-start.19 = (f16[48,384]{1,0:T(8,128)(2,1)S(1)}, f16[48,384]{1,0:T(8,128)(2,1)S(1)}, u32[]{:S(2)}, u32[]{:S(2)}) collective-permute-start(f16[48,384]{1,0:T(8,128)(2,1)S(1)} %convert_element_type.222), channel_id=1, source_target_pairs={{0,16},{1,17},{2,18},{3,19},{4,20},{5,21},{6,22},{7,23},{8,24},{9,... | collective-permute-start | bytes 110600 | tf_op jit(solution)/shard_map/ppermute | solution.py:308
  57.7 14.4 %collective-permute-start.20 = (f16[48,384]{1,0:T(8,128)(2,1)S(1)}, f16[48,384]{1,0:T(8,128)(2,1)S(1)}, u32[]{:S(2)}, u32[]{:S(2)}) collective-permute-start(f16[48,384]{1,0:T(8,128)(2,1)S(1)} %convert_element_type.225), channel_id=1, source_target_pairs={{0,24},{1,25},{2,26},{3,27},{4,28},{5,29},{6,30},{7,31},{8,0},{9,1... | collective-permute-start | bytes 110600 | tf_op jit(solution)/shard_map/ppermute | solution.py:308
  67.8 7.3 %collective-permute-start.6 = (f16[152,768]{1,0:T(8,128)(2,1)S(1)}, f16[152,768]{1,0:T(8,128)(2,1)S(1)}, u32[]{:S(2)}, u32[]{:S(2)}) collective-permute-start(f16[152,768]{1,0:T(8,128)(2,1)S(1)} %convert_element_type.183), channel_id=1, source_target_pairs={{0,32},{1,33},{2,10},{3,11},{4,36},{5,37},{6,14},{7,15},{8,40},{9,... | collective-permute-start | bytes 700424 | tf_op jit(solution)/shard_map/ppermute | solution.py:308
  68.9 9.6 %collective-permute-start.7 = (f16[152,768]{1,0:T(8,128)(2,1)S(1)}, f16[152,768]{1,0:T(8,128)(2,1)S(1)}, u32[]{:S(2)}, u32[]{:S(2)}) collective-permute-start(f16[152,768]{1,0:T(8,128)(2,1)S(1)} %convert_element_type.186), channel_id=1, source_target_pairs={{0,64},{1,65},{2,18},{3,19},{4,68},{5,69},{6,22},{7,23},{8,72},{9,... | collective-permute-start | bytes 700424 | tf_op jit(solution)/shard_map/ppermute | solution.py:308
  72.1 6.5 %collective-permute-start.8 = (f16[152,768]{1,0:T(8,128)(2,1)S(1)}, f16[152,768]{1,0:T(8,128)(2,1)S(1)}, u32[]{:S(2)}, u32[]{:S(2)}) collective-permute-start(f16[152,768]{1,0:T(8,128)(2,1)S(1)} %convert_element_type.189), channel_id=1, source_target_pairs={{0,96},{1,97},{2,26},{3,27},{4,100},{5,101},{6,30},{7,31},{8,104},... | collective-permute-start | bytes 700424 | tf_op jit(solution)/shard_map/ppermute | solution.py:308
  79.5 6.0 %collective-permute-start.10 = (f16[48,768]{1,0:T(8,128)(2,1)S(1)}, f16[48,768]{1,0:T(8,128)(2,1)S(1)}, u32[]{:S(2)}, u32[]{:S(2)}) collective-permute-start(f16[48,768]{1,0:T(8,128)(2,1)S(1)} %convert_element_type.195), channel_id=1, source_target_pairs={{0,4},{1,5},{2,66},{3,67},{4,0},{5,1},{6,70},{7,71},{8,12},{9,13},... | collective-permute-start | bytes 221192 | tf_op jit(solution)/shard_map/ppermute | solution.py:308
  80.3 6.0 %collective-permute-start.9 = (f16[48,768]{1,0:T(8,128)(2,1)S(1)}, f16[48,768]{1,0:T(8,128)(2,1)S(1)}, u32[]{:S(2)}, u32[]{:S(2)}) collective-permute-start(f16[48,768]{1,0:T(8,128)(2,1)S(1)} %convert_element_type.192), channel_id=1, source_target_pairs={{0,1},{1,4},{2,34},{3,35},{4,5},{5,0},{6,38},{7,39},{8,9},{9,12},{... | collective-permute-start | bytes 221192 | tf_op jit(solution)/shard_map/ppermute | solution.py:308
  81.0 5.3 %collective-permute-start.11 = (f16[48,768]{1,0:T(8,128)(2,1)S(1)}, f16[48,768]{1,0:T(8,128)(2,1)S(1)}, u32[]{:S(2)}, u32[]{:S(2)}) collective-permute-start(f16[48,768]{1,0:T(8,128)(2,1)S(1)} %convert_element_type.198), channel_id=1, source_target_pairs={{0,5},{1,0},{2,98},{3,99},{4,1},{5,4},{6,102},{7,103},{8,13},{9,8}... | collective-permute-start | bytes 221192 | tf_op jit(solution)/shard_map/ppermute | solution.py:308

commit v2 on v1

--- a/solution.py
+++ b/solution.py
@@ -17,7 +17,7 @@
 FIRST = {"wide": "xy", "narrow": "zz"}
 SECOND = {"wide": "zx", "narrow": "yy"}
 THIRD = {"wide": "yz", "narrow": "xx"}
-PARTS = ("wide", "narrow")
+PARTS = ("narrow", "wide")
 WIDE = 768
 NARROW = 384
 
@@ -263,10 +263,11 @@
     else:
         at = jnp.where(swap, y, z) if part == "wide" else x
         major, minor = 1, 0
-    outs, level, scratch = refs[0:4], refs[4], refs[5]
+    outs, level, scratch = refs[0:4], refs[4:-1], refs[-1]
     width = value.shape[1]
     bits = jnp.minimum(jnp.min(tails[...], axis=0, keepdims=True), before[0:1]) - 2.0
-    level[...] = jnp.broadcast_to(bits, (TAIL, 128))
+    if level:
+        level[0][...] = jnp.broadcast_to(bits, (TAIL, 128))
     scale = jnp.exp2(bits)[0:1, 0:1]
     for i in range(blocks):
         scratch[i, 0:BLOCK] = value[BLOCK * i : BLOCK * (i + 1)]
@@ -291,15 +292,15 @@
     out = pl.pallas_call(
         functools.partial(spread_body, part, kept, blocks),
         in_specs=[pl.BlockSpec(memory_space=pltpu.SMEM)] + [pl.BlockSpec(memory_space=pltpu.VMEM)] * 3,
-        out_specs=[pl.BlockSpec(memory_space=pltpu.VMEM)] * 5,
+        out_specs=[pl.BlockSpec(memory_space=pltpu.VMEM)] * (5 if blocks > SIDE else 4),
         out_shape=[pltpu.VMEM((kept, width), jnp.float32)]
         + [pltpu.VMEM((kept + TAIL, width), jnp.float32)] * 3
-        + [pltpu.VMEM((TAIL, 128), jnp.float32)],
+        + [pltpu.VMEM((TAIL, 128), jnp.float32)] * (blocks > SIDE),
         scratch_shapes=[pltpu.VMEM((blocks, PADDED, width), jnp.float32)],
         compiler_params=pltpu.CompilerParams(vmem_limit_bytes=12 * 2**20),
         cost_estimate=pl.CostEstimate(flops=10**8, bytes_accessed=10**7, transcendentals=0),
     )(where, *map(near, inputs))
-    return out[:4], out[4]
+    return out[:4], out[4:]
 
 
 def exchange(chunks, dims):
@@ -369,35 +370,34 @@
     got_two = across_cores(send_two)
     kept, got = (keep_one, keep_two), (got_one, got_two)
 
-    early = (("wide", 1), ("wide", 3), ("narrow", 1), ("narrow", 3))
+    early = (("narrow", 1), ("narrow", 3), ("wide", 1), ("wide", 3))
     *sums, bounds = product(early, where, kept, [out_grad], "bounds", [top, other_grad])
-    arrived = {"wide": {}, "narrow": {}}
+    arrived = {part: {} for part in PARTS}
     level = None
-    for jobs, started in ((early[:1], sums[:1]), (early[1:2], sums[1:2]), (early[2:], sums[2:])):
+    for jobs, started in ((early[:2], sums[:2]), (early[2:3], sums[2:3]), (early[3:], sums[3:])):
         if level is None:
-            value, level = product(jobs, where, got, [other_grad], "make", [bounds], started)
-            values = [value]
+            *values, level = product(jobs, where, got, [other_grad], "make", [bounds], started)
         else:
             values = product(jobs, where, got, [other_grad], "use", [level], started)
         for (part, k), value in zip(jobs, values):
             arrived[part] |= exchange({k: value}, FIRST[part])
     both, grads = (*kept, *got), [out_grad, other_grad]
-    jobs = (("wide", 2), ("narrow", 2))
+    jobs = tuple((part, 2) for part in PARTS)
     values = product(jobs, where, both, grads, "use", [level])
     for (part, k), value in zip(jobs, values):
         arrived[part] |= exchange({k: value}, FIRST[part])
 
     hidden_grad = input_gradient(out_grad, down_weight)
-    stay = product((("wide", 0), ("narrow", 0)), where, both, grads, "use", [level])
-
-    columns = []
+    stay = product(tuple((part, 0) for part in PARTS), where, both, grads, "use", [level])
+
+    columns = {}
     for part, own in zip(PARTS, stay):
-        (own, *chunks), bits = spread(where, part, 16, own, listed(arrived[part]), level)
+        (own, *chunks), (bits,) = spread(where, part, 16, own, listed(arrived[part]), level)
         parts = exchange({k: chunks[k - 1] for k in LATE}, SECOND[part])
-        (own, *chunks), bits = spread(where, part, 4, own, listed(parts), bits)
+        (own, *chunks), _ = spread(where, part, 4, own, listed(parts), bits)
         parts = exchange({k: chunks[k - 1] for k in LATE}, THIRD[part])
-        columns.append(total(own, listed(parts), PADDED)[0:BLOCK])
-    weight_grad = jnp.concatenate(columns, 1) * factor
+        columns[part] = total(own, listed(parts), PADDED)[0:BLOCK]
+    weight_grad = jnp.concatenate([columns["wide"], columns["narrow"]], 1) * factor
     return (weight_grad, hidden_grad)
 
 

time: 87.2 us -> 87.4 us (level)
  the two profiles are of different devices: /device:TPU:0 before, /device:TPU:2 now
where the time goes in v2:
time: 87.4 us; the launch traced here: 87.3 us
  starting transfers between devices  32.2 us (37%)
  waiting for transfers between devices  31.5 us (36%)
  Pallas kernels  19.2 us (22%)
  other arithmetic  3.02 us (3%)
  between operations  1.12 us (1%)
    ppermute x18, starting transfers between devices, exchange(): lax.ppermute(chunks[k].astype(jnp.float16), AXES, routes(dims, k))  31.4 us
    ppermute x18, waiting for transfers between devices, exchange(): lax.ppermute(chunks[k].astype(jnp.float16), AXES, routes(dims, k))  29.1 us
    pallas_call x1, Pallas kernels, input_gradient(): pl.pallas_call(input_gradient_body, in_specs=[pl.BlockSpec(memory_space=p...  8.55 us
    pallas_call x6, Pallas kernels, product(): pl.pallas_call(functools.partial(product_body, jobs, len(sources), len(we...  6.57 us
    pallas_call x1, Pallas kernels, turn_first(): pl.pallas_call(functools.partial(turn_first_body, tokens), in_specs=[pl.B...  2.5 us
    ppermute x3, waiting for transfers between devices, across_cores(): return lax.ppermute(array, AXES, pairs)  2.43 us
  transfers between devices with their start and end apart: 21, of which 9 were waited for; matrix products, arithmetic and copies ran while one was open for 2% of the time, Pallas kernels for 17%

profile of v2, /device:TPU:2, one launch (start us, length us, event | category | flops | bytes accessed | tf_op | source)
XLA Modules:
  0.0 87.3 jit_solution(15870469018569176726)
XLA Ops:
  0.6 2.5 %shard_map.50 = (bf16[4,576,256]{2,1,0:T(8,128)(2,1)S(1)}, bf16[4,576,256]{2,1,0:T(8,128)(2,1)S(1)}, bf16[4,128,1152]{2,1,0:T(8,128)(2,1)S(1)}, f32[8,128]{1,0:T(8,128)S(1)}) custom-call(s32[1]{0:T(128)} %bitcast.where, bf16[384,4608]{1,0:T(8,128)(2,1)} %hidden.1), custom_call_target="tpu_custom_call" | custom-call | flops 1000000000 | bytes 4000000 | tf_op jit(solution)/shard_map/pallas_call | solution.py:121
  3.8 0.9 %shard_map.51 = (bf16[4,584,128]{2,1,0:T(8,128)(2,1)S(1)}, bf16[4,576,128]{2,1,0:T(8,128)(2,1)S(1)}, f32[8,128]{1,0:T(8,128)S(1)}) custom-call(s32[1]{0:T(128)} %bitcast.where, bf16[4,128,1152]{2,1,0:T(8,128)(2,1)S(1)} %get-tuple-element.40.rest, f32[8,128]{1,0:T(8,128)S(1)} %get-tuple-element.41.before), custom_call_target="tpu_custom_call" | custom-call | flops 1000000000 | bytes 4000000 | tf_op jit(solution)/shard_map/pallas_call | solution.py:156
  4.9 2.4 %collective-permute-done.2.refs_4_.refs_2_.refs_5_ = bf16[384,1152]{1,0:T(8,128)(2,1)S(1)} collective-permute-done((bf16[384,1152]{1,0:T(8,128)(2,1)S(1)}, bf16[384,1152]{1,0:T(8,128)(2,1)S(1)}, u32[]{:S(2)}, u32[]{:S(2)}) %collective-permute-start.2) | collective-permute-done | bytes 884768 | tf_op jit(solution)/shard_map/ppermute | solution.py:52
  7.4 1.9 %shard_map.52 = (f32[576,384]{1,0:T(8,128)S(1)}, f32[576,384]{1,0:T(8,128)S(1)}, f32[576,768]{1,0:T(8,128)S(1)}, f32[576,768]{1,0:T(8,128)S(1)}, f32[16,128]{1,0:T(8,128)S(1)}) custom-call(s32[1]{0:T(128)} %bitcast.where, bf16[4,576,256]{2,1,0:T(8,128)(2,1)S(1)} %get-tuple-element.39.refs_0_, bf16[4,576,128]{2,1,0:T(8,128)(2,1)S(1)} %get-tuple-element.42.refs_1_, ...), custom_call_target="tpu_custom_call" | custom-call | flops 1019215872 | bytes 1000000 | tf_op jit(solution)/shard_map/pallas_call | solution.py:235
  9.3 0.7 shard_map.53
  10.0 1.4 %shard_map.56 = (f32[584,384]{1,0:T(8,128)S(1)}, f32[584,768]{1,0:T(8,128)S(1)}) custom-call(s32[1]{0:T(128)} %bitcast.where, bf16[4,576,256]{2,1,0:T(8,128)(2,1)S(1)} %get-tuple-element.39.refs_0_, bf16[4,576,128]{2,1,0:T(8,128)(2,1)S(1)} %get-tuple-element.42.refs_1_, bf16[4,576,256]{2,1,0:T(8,128)(2,1)S(1)} %collective-permute-done.refs_0_.refs_2_, ...), custom_call_target="tpu_custom_call" | custom-call | flops 1019215872 | bytes 1000000 | tf_op jit(solution)/shard_map/pallas_call | solution.py:235
  11.4 4.0 %collective-permute-start.13 = (f16[584,384]{1,0:T(8,128)(2,1)S(1)}, f16[584,384]{1,0:T(8,128)(2,1)S(1)}, u32[]{:S(2)}, u32[]{:S(2)}) collective-permute-start(f16[584,384]{1,0:T(8,128)(2,1)S(1)} %convert_element_type.204), channel_id=1, source_target_pairs={{0,64},{1,65},{2,66},{3,67},{4,68},{5,69},{6,70},{7,71},{8,72},{9,... | collective-permute-start | bytes 1345544 | tf_op jit(solution)/shard_map/ppermute | solution.py:309
  15.5 1.1 %collective-permute-start.12 = (f16[584,384]{1,0:T(8,128)(2,1)S(1)}, f16[584,384]{1,0:T(8,128)(2,1)S(1)}, u32[]{:S(2)}, u32[]{:S(2)}) collective-permute-start(f16[584,384]{1,0:T(8,128)(2,1)S(1)} %convert_element_type.201), channel_id=1, source_target_pairs={{0,32},{1,33},{2,34},{3,35},{4,36},{5,37},{6,38},{7,39},{8,40},{9,... | collective-permute-start | bytes 1345544 | tf_op jit(solution)/shard_map/ppermute | solution.py:309
  16.6 2.3 %collective-permute-start.14 = (f16[584,384]{1,0:T(8,128)(2,1)S(1)}, f16[584,384]{1,0:T(8,128)(2,1)S(1)}, u32[]{:S(2)}, u32[]{:S(2)}) collective-permute-start(f16[584,384]{1,0:T(8,128)(2,1)S(1)} %convert_element_type.207), channel_id=1, source_target_pairs={{0,96},{1,97},{2,98},{3,99},{4,100},{5,101},{6,102},{7,103},{8,104... | collective-permute-start | bytes 1345544 | tf_op jit(solution)/shard_map/ppermute | solution.py:309
  18.9 0.6 shard_map.55
  19.7 1.6 %collective-permute-start.3 = (f16[584,768]{1,0:T(8,128)(2,1)S(1)}, f16[584,768]{1,0:T(8,128)(2,1)S(1)}, u32[]{:S(2)}, u32[]{:S(2)}) collective-permute-start(f16[584,768]{1,0:T(8,128)(2,1)S(1)} %convert_element_type.174), channel_id=1, source_target_pairs={{0,8},{1,9},{2,3},{3,6},{4,12},{5,13},{6,7},{7,2},{8,16},{9,17},{1... | collective-permute-start | bytes 2691080 | tf_op jit(solution)/shard_map/ppermute | solution.py:309
  21.2 0.6 shard_map.57
  22.0 0.6 collective-permute-start.5
  22.6 1.3 %shard_map.54 = (f32[576,384]{1,0:T(8,128)S(1)}, f32[576,768]{1,0:T(8,128)S(1)}) custom-call(s32[1]{0:T(128)} %bitcast.where, bf16[4,576,256]{2,1,0:T(8,128)(2,1)S(1)} %get-tuple-element.39.refs_0_, bf16[4,576,128]{2,1,0:T(8,128)(2,1)S(1)} %get-tuple-element.42.refs_1_, bf16[4,576,256]{2,1,0:T(8,128)(2,1)S(1)} %collective-permute-done.refs_0_.refs_2_, ...), custom_call_target="tpu_custom_call" | custom-call | flops 1019215872 | bytes 1000000 | tf_op jit(solution)/shard_map/pallas_call | solution.py:235
  23.9 2.7 %collective-permute-done.13 = f16[584,384]{1,0:T(8,128)(2,1)S(1)} collective-permute-done((f16[584,384]{1,0:T(8,128)(2,1)S(1)}, f16[584,384]{1,0:T(8,128)(2,1)S(1)}, u32[]{:S(2)}, u32[]{:S(2)}) %collective-permute-start.13) | collective-permute-done | bytes 448544 | tf_op jit(solution)/shard_map/ppermute | solution.py:309
  26.6 9.0 %collective-permute-done.12 = f16[584,384]{1,0:T(8,128)(2,1)S(1)} collective-permute-done((f16[584,384]{1,0:T(8,128)(2,1)S(1)}, f16[584,384]{1,0:T(8,128)(2,1)S(1)}, u32[]{:S(2)}, u32[]{:S(2)}) %collective-permute-start.12) | collective-permute-done | bytes 448544 | tf_op jit(solution)/shard_map/ppermute | solution.py:309
  35.6 0.8 collective-permute-done.14
  37.0 1.6 %collective-permute-start.15 = (f16[152,384]{1,0:T(8,128)(2,1)S(1)}, f16[152,384]{1,0:T(8,128)(2,1)S(1)}, u32[]{:S(2)}, u32[]{:S(2)}) collective-permute-start(f16[152,384]{1,0:T(8,128)(2,1)S(1)} %convert_element_type.210), channel_id=1, source_target_pairs={{0,1},{1,4},{2,3},{3,6},{4,5},{5,0},{6,7},{7,2},{8,9},{9,12},{10,1... | collective-permute-start | bytes 350216 | tf_op jit(solution)/shard_map/ppermute | solution.py:309
  38.6 3.0 %collective-permute-start.16 = (f16[152,384]{1,0:T(8,128)(2,1)S(1)}, f16[152,384]{1,0:T(8,128)(2,1)S(1)}, u32[]{:S(2)}, u32[]{:S(2)}) collective-permute-start(f16[152,384]{1,0:T(8,128)(2,1)S(1)} %convert_element_type.213), channel_id=1, source_target_pairs={{0,4},{1,5},{2,6},{3,7},{4,0},{5,1},{6,2},{7,3},{8,12},{9,13},{10,... | collective-permute-start | bytes 350216 | tf_op jit(solution)/shard_map/ppermute | solution.py:309
  41.6 1.6 %collective-permute-start.17 = (f16[152,384]{1,0:T(8,128)(2,1)S(1)}, f16[152,384]{1,0:T(8,128)(2,1)S(1)}, u32[]{:S(2)}, u32[]{:S(2)}) collective-permute-start(f16[152,384]{1,0:T(8,128)(2,1)S(1)} %convert_element_type.216), channel_id=1, source_target_pairs={{0,5},{1,0},{2,7},{3,2},{4,1},{5,4},{6,3},{7,6},{8,13},{9,8},{10,1... | collective-permute-start | bytes 350216 | tf_op jit(solution)/shard_map/ppermute | solution.py:309
  43.2 8.6 %shard_map.62 = bf16[384,4608]{1,0:T(8,128)(2,1)} custom-call(bf16[384,1152]{1,0:T(8,128)(2,1)S(1)} %copy-done, bf16[4608,1152]{1,0:T(8,128)(2,1)} %weight.1), custom_call_target="tpu_custom_call" | custom-call | flops 4076863488 | bytes 15000000 | tf_op jit(solution)/shard_map/pallas_call | solution.py:339
  51.9 2.2 %collective-permute-start.4 = (f16[584,768]{1,0:T(8,128)(2,1)S(1)}, f16[584,768]{1,0:T(8,128)(2,1)S(1)}, u32[]{:S(2)}, u32[]{:S(2)}) collective-permute-start(f16[584,768]{1,0:T(8,128)(2,1)S(1)} %convert_element_type.177), channel_id=1, source_target_pairs={{0,16},{1,17},{2,6},{3,7},{4,20},{5,21},{6,2},{7,3},{8,24},{9,25},... | collective-permute-start | bytes 2691080 | tf_op jit(solution)/shard_map/ppermute | solution.py:309
  54.5 3.6 %collective-permute-start.19 = (f16[48,384]{1,0:T(8,128)(2,1)S(1)}, f16[48,384]{1,0:T(8,128)(2,1)S(1)}, u32[]{:S(2)}, u32[]{:S(2)}) collective-permute-start(f16[48,384]{1,0:T(8,128)(2,1)S(1)} %convert_element_type.222), channel_id=1, source_target_pairs={{0,16},{1,17},{2,18},{3,19},{4,20},{5,21},{6,22},{7,23},{8,24},{9,... | collective-permute-start | bytes 110600 | tf_op jit(solution)/shard_map/ppermute | solution.py:309
  58.8 8.1 %collective-permute-done.4 = f16[584,768]{1,0:T(8,128)(2,1)S(1)} collective-permute-done((f16[584,768]{1,0:T(8,128)(2,1)S(1)}, f16[584,768]{1,0:T(8,128)(2,1)S(1)}, u32[]{:S(2)}, u32[]{:S(2)}) %collective-permute-start.4) | collective-permute-done | bytes 897056 | tf_op jit(solution)/shard_map/ppermute | solution.py:309
  67.9 1.3 %collective-permute-start.6 = (f16[152,768]{1,0:T(8,128)(2,1)S(1)}, f16[152,768]{1,0:T(8,128)(2,1)S(1)}, u32[]{:S(2)}, u32[]{:S(2)}) collective-permute-start(f16[152,768]{1,0:T(8,128)(2,1)S(1)} %convert_element_type.183), channel_id=1, source_target_pairs={{0,32},{1,33},{2,10},{3,11},{4,36},{5,37},{6,14},{7,15},{8,40},{9,... | collective-permute-start | bytes 700424 | tf_op jit(solution)/shard_map/ppermute | solution.py:309
  69.2 3.6 %collective-permute-start.7 = (f16[152,768]{1,0:T(8,128)(2,1)S(1)}, f16[152,768]{1,0:T(8,128)(2,1)S(1)}, u32[]{:S(2)}, u32[]{:S(2)}) collective-permute-start(f16[152,768]{1,0:T(8,128)(2,1)S(1)} %convert_element_type.186), channel_id=1, source_target_pairs={{0,64},{1,65},{2,18},{3,19},{4,68},{5,69},{6,22},{7,23},{8,72},{9,... | collective-permute-start | bytes 700424 | tf_op jit(solution)/shard_map/ppermute | solution.py:309
  73.6 1.7 %collective-permute-done.6 = f16[152,768]{1,0:T(8,128)(2,1)S(1)} collective-permute-done((f16[152,768]{1,0:T(8,128)(2,1)S(1)}, f16[152,768]{1,0:T(8,128)(2,1)S(1)}, u32[]{:S(2)}, u32[]{:S(2)}) %collective-permute-start.6) | collective-permute-done | bytes 233504 | tf_op jit(solution)/shard_map/ppermute | solution.py:309
  75.3 4.0 %collective-permute-done.7 = f16[152,768]{1,0:T(8,128)(2,1)S(1)} collective-permute-done((f16[152,768]{1,0:T(8,128)(2,1)S(1)}, f16[152,768]{1,0:T(8,128)(2,1)S(1)}, u32[]{:S(2)}, u32[]{:S(2)}) %collective-permute-start.7) | collective-permute-done | bytes 233504 | tf_op jit(solution)/shard_map/ppermute | solution.py:309
  80.8 2.8 %collective-permute-start.11 = (f16[48,768]{1,0:T(8,128)(2,1)S(1)}, f16[48,768]{1,0:T(8,128)(2,1)S(1)}, u32[]{:S(2)}, u32[]{:S(2)}) collective-permute-start(f16[48,768]{1,0:T(8,128)(2,1)S(1)} %convert_element_type.198), channel_id=1, source_target_pairs={{0,5},{1,0},{2,98},{3,99},{4,1},{5,4},{6,102},{7,103},{8,13},{9,8}... | collective-permute-start | bytes 221192 | tf_op jit(solution)/shard_map/ppermute | solution.py:309
  83.5 2.1 %collective-permute-done.10 = f16[48,768]{1,0:T(8,128)(2,1)S(1)} collective-permute-done((f16[48,768]{1,0:T(8,128)(2,1)S(1)}, f16[48,768]{1,0:T(8,128)(2,1)S(1)}, u32[]{:S(2)}, u32[]{:S(2)}) %collective-permute-start.10) | collective-permute-done | bytes 73760 | tf_op jit(solution)/shard_map/ppermute | solution.py:309
  85.7 0.7 collective-permute-done.9
  86.6 0.7 maximum_multiply_fusion
  (90 shorter events, 6.2 us)
Async XLA Ops:
  0.6 2.6 %copy-start = (bf16[384,1152]{1,0:T(8,128)(2,1)S(1)}, bf16[384,1152]{1,0:T(8,128)(2,1)}, u32[]{:S(2)}) copy-start(bf16[384,1152]{1,0:T(8,128)(2,1)} %grad.1) | copy-start | bytes 2654212
  3.2 6.1 %collective-permute-start = (bf16[4,576,256]{2,1,0:T(8,128)(2,1)S(1)}, bf16[4,576,256]{2,1,0:T(8,128)(2,1)S(1)}, u32[]{:S(2)}, u32[]{:S(2)}) collective-permute-start(bf16[4,576,256]{2,1,0:T(8,128)(2,1)S(1)} %get-tuple-element.43), channel_id=1, source_target_pairs={{0,2},{1,3},{2,0},{3,1},{4,6},{5,7},{6,4},{7,5},{8,10},{9,11},{10,... | collective-permute-start | bytes 3538952 | tf_op jit(solution)/shard_map/ppermute | solution.py:52
  3.3 4.1 %collective-permute-start.2 = (bf16[384,1152]{1,0:T(8,128)(2,1)S(1)}, bf16[384,1152]{1,0:T(8,128)(2,1)S(1)}, u32[]{:S(2)}, u32[]{:S(2)}) collective-permute-start(bf16[384,1152]{1,0:T(8,128)(2,1)S(1)} %copy-done), channel_id=1, source_target_pairs={{0,2},{1,3},{2,0},{3,1},{4,6},{5,7},{6,4},{7,5},{8,10},{9,11},{10,... | collective-permute-start | bytes 2654216 | tf_op jit(solution)/shard_map/ppermute | solution.py:52
  4.7 4.6 %collective-permute-start.1 = (bf16[4,584,128]{2,1,0:T(8,128)(2,1)S(1)}, bf16[4,584,128]{2,1,0:T(8,128)(2,1)S(1)}, u32[]{:S(2)}, u32[]{:S(2)}) collective-permute-start(bf16[4,584,128]{2,1,0:T(8,128)(2,1)S(1)} %get-tuple-element.44), channel_id=1, source_target_pairs={{0,2},{1,3},{2,0},{3,1},{4,6},{5,7},{6,4},{7,5},{8,10},{9,11},{10,... | collective-permute-start | bytes 1794056 | tf_op jit(solution)/shard_map/ppermute | solution.py:52
  11.4 15.2 %collective-permute-start.13 = (f16[584,384]{1,0:T(8,128)(2,1)S(1)}, f16[584,384]{1,0:T(8,128)(2,1)S(1)}, u32[]{:S(2)}, u32[]{:S(2)}) collective-permute-start(f16[584,384]{1,0:T(8,128)(2,1)S(1)} %convert_element_type.204), channel_id=1, source_target_pairs={{0,64},{1,65},{2,66},{3,67},{4,68},{5,69},{6,70},{7,71},{8,72},{9,... | collective-permute-start | bytes 1345544 | tf_op jit(solution)/shard_map/ppermute | solution.py:309
  15.5 20.2 %collective-permute-start.12 = (f16[584,384]{1,0:T(8,128)(2,1)S(1)}, f16[584,384]{1,0:T(8,128)(2,1)S(1)}, u32[]{:S(2)}, u32[]{:S(2)}) collective-permute-start(f16[584,384]{1,0:T(8,128)(2,1)S(1)} %convert_element_type.201), channel_id=1, source_target_pairs={{0,32},{1,33},{2,34},{3,35},{4,36},{5,37},{6,38},{7,39},{8,40},{9,... | collective-permute-start | bytes 1345544 | tf_op jit(solution)/shard_map/ppermute | solution.py:309
  16.6 19.8 %collective-permute-start.14 = (f16[584,384]{1,0:T(8,128)(2,1)S(1)}, f16[584,384]{1,0:T(8,128)(2,1)S(1)}, u32[]{:S(2)}, u32[]{:S(2)}) collective-permute-start(f16[584,384]{1,0:T(8,128)(2,1)S(1)} %convert_element_type.207), channel_id=1, source_target_pairs={{0,96},{1,97},{2,98},{3,99},{4,100},{5,101},{6,102},{7,103},{8,104... | collective-permute-start | bytes 1345544 | tf_op jit(solution)/shard_map/ppermute | solution.py:309
  19.7 38.5 %collective-permute-start.3 = (f16[584,768]{1,0:T(8,128)(2,1)S(1)}, f16[584,768]{1,0:T(8,128)(2,1)S(1)}, u32[]{:S(2)}, u32[]{:S(2)}) collective-permute-start(f16[584,768]{1,0:T(8,128)(2,1)S(1)} %convert_element_type.174), channel_id=1, source_target_pairs={{0,8},{1,9},{2,3},{3,6},{4,12},{5,13},{6,7},{7,2},{8,16},{9,17},{1... | collective-permute-start | bytes 2691080 | tf_op jit(solution)/shard_map/ppermute | solution.py:309
  22.0 36.8 %collective-permute-start.5 = (f16[584,768]{1,0:T(8,128)(2,1)S(1)}, f16[584,768]{1,0:T(8,128)(2,1)S(1)}, u32[]{:S(2)}, u32[]{:S(2)}) collective-permute-start(f16[584,768]{1,0:T(8,128)(2,1)S(1)} %convert_element_type.180), channel_id=1, source_target_pairs={{0,24},{1,25},{2,7},{3,2},{4,28},{5,29},{6,3},{7,6},{8,0},{9,1},{1... | collective-permute-start | bytes 2691080 | tf_op jit(solution)/shard_map/ppermute | solution.py:309
  37.0 14.9 %collective-permute-start.15 = (f16[152,384]{1,0:T(8,128)(2,1)S(1)}, f16[152,384]{1,0:T(8,128)(2,1)S(1)}, u32[]{:S(2)}, u32[]{:S(2)}) collective-permute-start(f16[152,384]{1,0:T(8,128)(2,1)S(1)} %convert_element_type.210), channel_id=1, source_target_pairs={{0,1},{1,4},{2,3},{3,6},{4,5},{5,0},{6,7},{7,2},{8,9},{9,12},{10,1... | collective-permute-start | bytes 350216 | tf_op jit(solution)/shard_map/ppermute | solution.py:309
  38.6 15.5 %collective-permute-start.16 = (f16[152,384]{1,0:T(8,128)(2,1)S(1)}, f16[152,384]{1,0:T(8,128)(2,1)S(1)}, u32[]{:S(2)}, u32[]{:S(2)}) collective-permute-start(f16[152,384]{1,0:T(8,128)(2,1)S(1)} %convert_element_type.213), channel_id=1, source_target_pairs={{0,4},{1,5},{2,6},{3,7},{4,0},{5,1},{6,2},{7,3},{8,12},{9,13},{10,... | collective-permute-start | bytes 350216 | tf_op jit(solution)/shard_map/ppermute | solution.py:309
  41.6 12.5 %collective-permute-start.17 = (f16[152,384]{1,0:T(8,128)(2,1)S(1)}, f16[152,384]{1,0:T(8,128)(2,1)S(1)}, u32[]{:S(2)}, u32[]{:S(2)}) collective-permute-start(f16[152,384]{1,0:T(8,128)(2,1)S(1)} %convert_element_type.216), channel_id=1, source_target_pairs={{0,5},{1,0},{2,7},{3,2},{4,1},{5,4},{6,3},{7,6},{8,13},{9,8},{10,1... | collective-permute-start | bytes 350216 | tf_op jit(solution)/shard_map/ppermute | solution.py:309
  51.9 15.0 %collective-permute-start.4 = (f16[584,768]{1,0:T(8,128)(2,1)S(1)}, f16[584,768]{1,0:T(8,128)(2,1)S(1)}, u32[]{:S(2)}, u32[]{:S(2)}) collective-permute-start(f16[584,768]{1,0:T(8,128)(2,1)S(1)} %convert_element_type.177), channel_id=1, source_target_pairs={{0,16},{1,17},{2,6},{3,7},{4,20},{5,21},{6,2},{7,3},{8,24},{9,25},... | collective-permute-start | bytes 2691080 | tf_op jit(solution)/shard_map/ppermute | solution.py:309
  54.4 19.0 %collective-permute-start.18 = (f16[48,384]{1,0:T(8,128)(2,1)S(1)}, f16[48,384]{1,0:T(8,128)(2,1)S(1)}, u32[]{:S(2)}, u32[]{:S(2)}) collective-permute-start(f16[48,384]{1,0:T(8,128)(2,1)S(1)} %convert_element_type.219), channel_id=1, source_target_pairs={{0,8},{1,9},{2,10},{3,11},{4,12},{5,13},{6,14},{7,15},{8,16},{9,17... | collective-permute-start | bytes 110600 | tf_op jit(solution)/shard_map/ppermute | solution.py:309
  54.5 18.9 %collective-permute-start.19 = (f16[48,384]{1,0:T(8,128)(2,1)S(1)}, f16[48,384]{1,0:T(8,128)(2,1)S(1)}, u32[]{:S(2)}, u32[]{:S(2)}) collective-permute-start(f16[48,384]{1,0:T(8,128)(2,1)S(1)} %convert_element_type.222), channel_id=1, source_target_pairs={{0,16},{1,17},{2,18},{3,19},{4,20},{5,21},{6,22},{7,23},{8,24},{9,... | collective-permute-start | bytes 110600 | tf_op jit(solution)/shard_map/ppermute | solution.py:309
  58.1 14.7 %collective-permute-start.20 = (f16[48,384]{1,0:T(8,128)(2,1)S(1)}, f16[48,384]{1,0:T(8,128)(2,1)S(1)}, u32[]{:S(2)}, u32[]{:S(2)}) collective-permute-start(f16[48,384]{1,0:T(8,128)(2,1)S(1)} %convert_element_type.225), channel_id=1, source_target_pairs={{0,24},{1,25},{2,26},{3,27},{4,28},{5,29},{6,30},{7,31},{8,0},{9,1... | collective-permute-start | bytes 110600 | tf_op jit(solution)/shard_map/ppermute | solution.py:309
  67.9 7.4 %collective-permute-start.6 = (f16[152,768]{1,0:T(8,128)(2,1)S(1)}, f16[152,768]{1,0:T(8,128)(2,1)S(1)}, u32[]{:S(2)}, u32[]{:S(2)}) collective-permute-start(f16[152,768]{1,0:T(8,128)(2,1)S(1)} %convert_element_type.183), channel_id=1, source_target_pairs={{0,32},{1,33},{2,10},{3,11},{4,36},{5,37},{6,14},{7,15},{8,40},{9,... | collective-permute-start | bytes 700424 | tf_op jit(solution)/shard_map/ppermute | solution.py:309
  69.2 10.1 %collective-permute-start.7 = (f16[152,768]{1,0:T(8,128)(2,1)S(1)}, f16[152,768]{1,0:T(8,128)(2,1)S(1)}, u32[]{:S(2)}, u32[]{:S(2)}) collective-permute-start(f16[152,768]{1,0:T(8,128)(2,1)S(1)} %convert_element_type.186), channel_id=1, source_target_pairs={{0,64},{1,65},{2,18},{3,19},{4,68},{5,69},{6,22},{7,23},{8,72},{9,... | collective-permute-start | bytes 700424 | tf_op jit(solution)/shard_map/ppermute | solution.py:309
  72.9 6.4 %collective-permute-start.8 = (f16[152,768]{1,0:T(8,128)(2,1)S(1)}, f16[152,768]{1,0:T(8,128)(2,1)S(1)}, u32[]{:S(2)}, u32[]{:S(2)}) collective-permute-start(f16[152,768]{1,0:T(8,128)(2,1)S(1)} %convert_element_type.189), channel_id=1, source_target_pairs={{0,96},{1,97},{2,26},{3,27},{4,100},{5,101},{6,30},{7,31},{8,104},... | collective-permute-start | bytes 700424 | tf_op jit(solution)/shard_map/ppermute | solution.py:309
  79.7 6.0 %collective-permute-start.10 = (f16[48,768]{1,0:T(8,128)(2,1)S(1)}, f16[48,768]{1,0:T(8,128)(2,1)S(1)}, u32[]{:S(2)}, u32[]{:S(2)}) collective-permute-start(f16[48,768]{1,0:T(8,128)(2,1)S(1)} %convert_element_type.195), channel_id=1, source_target_pairs={{0,4},{1,5},{2,66},{3,67},{4,0},{5,1},{6,70},{7,71},{8,12},{9,13},... | collective-permute-start | bytes 221192 | tf_op jit(solution)/shard_map/ppermute | solution.py:309
  80.1 6.3 %collective-permute-start.9 = (f16[48,768]{1,0:T(8,128)(2,1)S(1)}, f16[48,768]{1,0:T(8,128)(2,1)S(1)}, u32[]{:S(2)}, u32[]{:S(2)}) collective-permute-start(f16[48,768]{1,0:T(8,128)(2,1)S(1)} %convert_element_type.192), channel_id=1, source_target_pairs={{0,1},{1,4},{2,34},{3,35},{4,5},{5,0},{6,38},{7,39},{8,9},{9,12},{... | collective-permute-start | bytes 221192 | tf_op jit(solution)/shard_map/ppermute | solution.py:309
  80.8 5.7 %collective-permute-start.11 = (f16[48,768]{1,0:T(8,128)(2,1)S(1)}, f16[48,768]{1,0:T(8,128)(2,1)S(1)}, u32[]{:S(2)}, u32[]{:S(2)}) collective-permute-start(f16[48,768]{1,0:T(8,128)(2,1)S(1)} %convert_element_type.198), channel_id=1, source_target_pairs={{0,5},{1,0},{2,98},{3,99},{4,1},{5,4},{6,102},{7,103},{8,13},{9,8}... | collective-permute-start | bytes 221192 | tf_op jit(solution)/shard_map/ppermute | solution.py:309
